TPU v7x, 16 devices: a whole 2x2x2 slice. The times are simulated.
16 devices in a mesh: rep: 2 (over z), fsdp: 8 (over y, x, core).
Axes of the slice: x: 2, y: 2, z: 2, core: 2. Of those that a mesh axis runs over, the one named last changes fastest.
Arguments:
- x_tokens: bfloat16 [512, 50, 1024], P(('rep', 'fsdp'))
- grad_z: bfloat16 [512, 50, 1024], P(('rep', 'fsdp'))
- w_qkv: float32 [1024, 3072], P('fsdp')
- b_qkv: float32 [3072], P('fsdp')
- w_out: float32 [1024, 1024], P('fsdp')
- w_up: float32 [1024, 4096], P('fsdp')
- b_up: float32 [4096], P('fsdp')
- w_down: float32 [4096, 1024], P('fsdp')
- vec_params: float32 [8, 1024], P(None, 'fsdp')
Outputs:
- output 1: bfloat16 [512, 50, 1024], P(('rep', 'fsdp'))
- output 2: bfloat16 [512, 50, 1024], P(('rep', 'fsdp'))
- output 3: float32 [1024, 3072], P('fsdp')
- output 4: float32 [3072], P('fsdp')
- output 5: float32 [1024, 1024], P('fsdp')
- output 6: float32 [1024, 4096], P('fsdp')
- output 7: float32 [4096], P('fsdp')
- output 8: float32 [4096, 1024], P('fsdp')
- output 9: float32 [8, 1024], P(None, 'fsdp')
All inputs are finite; a program needn't handle non-finite values.
Results may differ from a plain program's by a relative error of at most 0.02.
Values are sent between devices in bfloat16 or wider.
A program may use at most 1 GiB of HBM per device.

v0:
```python
import functools

import jax
import jax.numpy as jnp
from jax import lax
from jax.experimental import pallas as pl
from jax.experimental.layout import Layout, with_layout_constraint
from jax.experimental.pallas import tpu as pltpu
from jax.sharding import PartitionSpec as P


HEADS = 16
LN_EPS = 1e-5
SEQ = 50
D = 1024
FF = 4096
SEQS = 32
T = SEQS * SEQ
NS = 8
CHUNKS = 2
HALF = D // 2
FC = FF // NS // CHUNKS
GROUP = 8
ROWS = GROUP * SEQ
PAIR = 2 * SEQ
WIN = 112
SCALE = (D // HEADS) ** -0.5
NEG = -3.0e38
F32 = jnp.float32
BF16 = jnp.bfloat16

ERFC_P = 0.45
ERFC_Q = (0.25388532876968384, 0.25388315320014954, 0.22827185690402985, 0.1752501279115677, 0.11996052414178848,
          -0.0223874319344759, 0.14245237410068512, -0.30063509941101074, 0.19071702659130096, -0.041397832334041595)


def dot(a, b):
    return lax.dot_general(a, b, (((1,), (0,)), ((), ())), preferred_element_type=F32)


def dot_nt(a, b):
    return lax.dot_general(a, b, (((1,), (1,)), ((), ())), preferred_element_type=F32)


def dot_tn(a, b):
    return lax.dot_general(a, b, (((0,), (0,)), ((), ())), preferred_element_type=F32)


def gelu_and_slope(u):
    dens = jnp.exp(u * u * -0.5)
    t = 1.0 / (1.0 + (ERFC_P * 0.5 ** 0.5) * jnp.abs(u))
    q = jnp.full_like(t, ERFC_Q[-1])
    for coef in ERFC_Q[-2::-1]:
        q = q * t + coef
    half = (0.5 * dens) * (t * q)
    cdf = jnp.where(u > 0, 1.0 - half, half)
    return u * cdf, cdf + u * dens * 0.3989422804014327


def window_parts(j):
    start = 16 * ((PAIR * j) // 16)
    off = PAIR * j - start
    r = lax.broadcasted_iota(jnp.int32, (WIN, WIN), 0)
    c = lax.broadcasted_iota(jnp.int32, (WIN, WIN), 1)

    def seq_of(v):
        one = jnp.int32(1)
        zero = jnp.int32(0)
        return (jnp.where(v >= off, one, zero) + jnp.where(v >= off + SEQ, one, zero)
                + jnp.where(v >= off + PAIR, one, zero))

    bias = jnp.where(seq_of(r) == seq_of(c), 0.0, NEG)
    row = lax.broadcasted_iota(jnp.int32, (WIN, 128), 0)
    lane = lax.broadcasted_iota(jnp.int32, (WIN, 128), 1)
    inside = (row >= off) & (row < off + PAIR)
    return start, bias, inside, lane < 64


def softmax_rows(s, bias2):
    s = jnp.where(bias2 == 0.0, s, NEG)
    m = jnp.max(s, axis=1, keepdims=True)
    p = jnp.exp2((s - m) * (SCALE * 1.4426950408889634))
    return p * (1.0 / jnp.sum(p, axis=1, keepdims=True))


def attn_fwd_kernel(q_ref, k_ref, v_ref, o_ref):
    for j in range(ROWS // PAIR):
        start, bias, inside, even = window_parts(j)
        bias2 = jnp.concatenate([bias, bias], axis=0)
        m_even = jnp.where(even, 1.0, 0.0).astype(BF16)
        m_odd = jnp.where(even, 0.0, 1.0).astype(BF16)
        for hp in range(q_ref.shape[1] // 128):
            cols = slice(hp * 128, hp * 128 + 128)
            q = q_ref[start:start + WIN, cols]
            k = k_ref[start:start + WIN, cols]
            v = v_ref[start:start + WIN, cols]
            q2 = jnp.concatenate([q * m_even, q * m_odd], axis=0)
            p = softmax_rows(dot_nt(q2, k), bias2)
            o2 = dot(p.astype(BF16), v)
            o = jnp.where(inside, jnp.where(even, o2[:WIN], o2[WIN:]), 0.0).astype(BF16)
            if j:
                o_ref[start:start + 16, cols] += o[:16]
                o_ref[start + 16:start + WIN, cols] = o[16:]
            else:
                o_ref[start:start + WIN, cols] = o


def attn_bwd_kernel(q_ref, k_ref, v_ref, g_ref, d_ref, b_ref):
    parts = []
    for j in range(ROWS // PAIR):
        start, bias, inside, even = window_parts(j)
        one_even = jnp.where(even, 1.0, 0.0)
        parts.append((start, jnp.concatenate([bias, bias], axis=0), one_even.astype(BF16), (1.0 - one_even).astype(BF16),
                      jnp.where(inside, one_even, 0.0).astype(BF16), jnp.where(inside, 1.0 - one_even, 0.0).astype(BF16)))

    def head_pair(hp):
        cols = slice(hp * 128, hp * 128 + 128)
        sums = [jnp.zeros((1, 128), F32) for _ in range(3)]
        for j, (start, bias2, m_even, m_odd, g_even, g_odd) in enumerate(parts):
            q = q_ref[start:start + WIN, cols]
            k = k_ref[start:start + WIN, cols]
            v = v_ref[start:start + WIN, cols]
            g = g_ref[start:start + WIN, cols]
            q2 = jnp.concatenate([q * m_even, q * m_odd], axis=0)
            g2 = jnp.concatenate([g * g_even, g * g_odd], axis=0)
            p = softmax_rows(dot_nt(q2, k), bias2)
            dp = dot_nt(g2, v)
            ds = (p * (dp - jnp.sum(dp * p, axis=1, keepdims=True)) * SCALE).astype(BF16)
            dq2 = dot(ds, k)
            even = lax.broadcasted_iota(jnp.int32, (WIN, 128), 1) < 64
            dq = jnp.where(even, dq2[:WIN], dq2[WIN:])
            dk = dot_tn(ds, q2)
            dv = dot_tn(p.astype(BF16), g2)
            for i, val in enumerate((dq, dk, dv)):
                out = slice(hp * 128 + i * HALF, hp * 128 + i * HALF + 128)
                sums[i] = sums[i] + jnp.sum(val, axis=0, keepdims=True)
                val = val.astype(BF16)
                if j:
                    d_ref[start:start + 16, out] += val[:16]
                    d_ref[start + 16:start + WIN, out] = val[16:]
                else:
                    d_ref[start:start + WIN, out] = val
        for i in range(3):
            b_ref[0, :, hp * 128 + i * HALF:hp * 128 + i * HALF + 128] = sums[i]

    for hp in range(HALF // 128):
        head_pair(hp)


ATT_COLS = 256


def attn_forward(qkv):
    per = HALF // ATT_COLS
    spec = lambda part: pl.BlockSpec((ROWS, ATT_COLS), lambda g, c: (g, (c // per * 3 + part) * per + c % per))
    return pl.pallas_call(
        attn_fwd_kernel,
        grid=(T // ROWS, D // ATT_COLS),
        in_specs=[spec(0), spec(1), spec(2)],
        out_specs=pl.BlockSpec((ROWS, ATT_COLS), lambda g, c: (g, c)),
        out_shape=jax.ShapeDtypeStruct((T, D), BF16),
        compiler_params=pltpu.CompilerParams(dimension_semantics=("arbitrary", "arbitrary")),
        cost_estimate=pl.CostEstimate(flops=8_000_000_000, bytes_accessed=13_000_000, transcendentals=3_000_000),
        name="attn_fwd",
    )(qkv, qkv, qkv)


def attn_backward(qkv, d_heads, half):
    spec = lambda at: pl.BlockSpec((ROWS, HALF), lambda g: (g, at))
    return pl.pallas_call(
        attn_bwd_kernel,
        grid=(T // ROWS,),
        in_specs=[spec(3 * half), spec(3 * half + 1), spec(3 * half + 2), spec(half)],
        out_specs=[pl.BlockSpec((ROWS, 3 * HALF), lambda g: (g, 0)), pl.BlockSpec((1, 1, 3 * HALF), lambda g: (g, 0, 0))],
        out_shape=[jax.ShapeDtypeStruct((T, 3 * HALF), BF16), jax.ShapeDtypeStruct((T // ROWS, 1, 3 * HALF), F32)],
        compiler_params=pltpu.CompilerParams(dimension_semantics=("arbitrary",)),
        cost_estimate=pl.CostEstimate(flops=16_000_000_000, bytes_accessed=12_000_000, transcendentals=1_500_000),
        name="attn_bwd",
    )(qkv, qkv, qkv, d_heads)


MLP_ROWS = 400
BLK = 2 * FC


def mlp_kernel(h_ref, g_ref, ht_ref, gt_ref, w1_ref, wd_ref, b1_ref, m_ref, dh_ref,
               gw1_send, gw1_keep, gw2_send, gw2_keep, gb_ref, act_s, dpre_s, w2_ref):
    step = pl.program_id(0)
    core = lax.rem(lax.axis_index("fsdp"), 2)
    gb_ref[...] = jnp.zeros_like(gb_ref)
    for n in range(4):
        w2_ref[n * 128:(n + 1) * 128, :] = wd_ref[n // 2, :, n % 2 * D:(n % 2 + 1) * D]

    @pl.when(step == 0)
    def _():
        m_ref[...] = jnp.zeros_like(m_ref)
        dh_ref[...] = jnp.zeros_like(dh_ref)

    def rows_step(i, carry):
        rows = pl.ds(pl.multiple_of(i * MLP_ROWS, 16), MLP_ROWS)
        w1 = w1_ref[...].reshape(D, BLK)
        u = dot(h_ref[rows, :], w1) + b1_ref[...]
        d_act = dot_nt(g_ref[rows, :], w2_ref[...])
        act, slope = gelu_and_slope(u)
        act = act.astype(BF16)
        d_pre = d_act * slope
        gb_ref[...] += jnp.sum(d_pre, axis=0, keepdims=True)
        d_pre = d_pre.astype(BF16)
        act_s[rows, :] = act
        dpre_s[rows, :] = d_pre
        m_ref[rows, :] += dot(act, w2_ref[...])
        dh_ref[rows, :] += dot_nt(d_pre, w1)
        return carry

    lax.fori_loop(0, T // MLP_ROWS, rows_step, 0)

    def grad_step(i, carry):
        for side, out in ((1 - core, gw1_send), (core, gw1_keep)):
            rows = pl.ds(pl.multiple_of((2 * i + side) * 128, 128), 128)
            out[i] = dot(ht_ref[rows, :], dpre_s[...])
        rows = pl.ds(pl.multiple_of(i * 256, 256), 256)
        for side, out in ((1 - core, gw2_send), (core, gw2_keep)):
            out[0, rows, :] = dot(gt_ref[rows, :], act_s[:, pl.ds(pl.multiple_of(side * FC, FC), FC)])
        return carry

    lax.fori_loop(0, D // 256, grad_step, 0)


def mlp_chunk(h, g, ht, gt, weights, b1):
    cols = NS * FC
    once = pl.Buffered(1)
    whole = lambda shape: pl.BlockSpec(shape, lambda s: (0, 0), pipeline_mode=once)
    return pl.pallas_call(
        mlp_kernel,
        grid=(cols // BLK,),
        in_specs=[whole((T, D)), whole((T, D)), whole((D, T)), whole((D, T)),
                  pl.BlockSpec((NS, D // NS, BLK), lambda s: (0, 0, s)),
                  pl.BlockSpec((2, D // NS, cols), lambda s: (s, 1, 0)),
                  pl.BlockSpec((1, BLK), lambda s: (0, s))],
        out_specs=[whole((T, D)), whole((T, D)),
                   *[pl.BlockSpec((4, D // NS, BLK), lambda s: (0, 0, s))] * 2,
                   *[pl.BlockSpec((1, D, FC), lambda s: (s, 0, 0))] * 2,
                   pl.BlockSpec((1, BLK), lambda s: (0, s))],
        out_shape=[jax.ShapeDtypeStruct((T, D), F32), jax.ShapeDtypeStruct((T, D), F32),
                   *[jax.ShapeDtypeStruct((4, D // NS, cols), F32)] * 2, *[jax.ShapeDtypeStruct((4, D, FC), F32)] * 2,
                   jax.ShapeDtypeStruct((1, cols), F32)],
        scratch_shapes=[pltpu.VMEM((T, BLK), BF16), pltpu.VMEM((T, BLK), BF16), pltpu.VMEM((BLK, D), BF16)],
        compiler_params=pltpu.CompilerParams(dimension_semantics=("arbitrary",), vmem_limit_bytes=62 * 1024 * 1024),
        cost_estimate=pl.CostEstimate(flops=12 * T * D * cols, bytes_accessed=60_000_000, transcendentals=T * cols),
        name="mlp_fwd_bwd",
    )(h, g, ht, gt, weights, weights, b1)


POST_ROWS = 200


def post_kernel(m0_ref, m1_ref, d0_ref, d1_ref, x_ref, att_ref, g_ref, vec_ref, z_ref, res_ref, da_ref, sum_ref):
    row = lambda i: vec_ref[i:i + 1, :]
    att = att_ref[...]
    y = x_ref[...].astype(F32) + row(3) * att
    m = m0_ref[...] + m1_ref[...] + row(6)
    g = g_ref[...].astype(F32)
    z_ref[...] = (y + row(7) * m).astype(BF16)
    xhat, rstd = ln_stats(y)
    dh = d0_ref[...] + d1_ref[...]
    res = g + ln_back(xhat, rstd, dh * row(4))
    res_ref[...] = res
    da = res * row(3)
    da_ref[...] = da.astype(BF16)

    @pl.when(pl.program_id(0) == 0)
    def _():
        sum_ref[...] = jnp.zeros_like(sum_ref)

    for i, val in ((2, da), (3, res * att), (4, dh * xhat), (5, dh), (6, g * row(7)), (7, g * m)):
        sum_ref[i:i + 1, :] += jnp.sum(val, axis=0, keepdims=True)


def post_mlp(m0, m1, d0, d1, x, att, g, vec):
    rows = pl.BlockSpec((POST_ROWS, D), lambda i: (i, 0))
    fixed = pl.BlockSpec((8, D), lambda i: (0, 0))
    return pl.pallas_call(
        post_kernel,
        grid=(T // POST_ROWS,),
        in_specs=[rows] * 7 + [fixed],
        out_specs=[rows, rows, rows, fixed],
        out_shape=[jax.ShapeDtypeStruct((T, D), BF16), jax.ShapeDtypeStruct((T, D), F32), jax.ShapeDtypeStruct((T, D), BF16),
                   jax.ShapeDtypeStruct((8, D), F32)],
        compiler_params=pltpu.CompilerParams(dimension_semantics=("arbitrary",)),
        cost_estimate=pl.CostEstimate(flops=5_000_000_000, bytes_accessed=56_000_000, transcendentals=T),
        name="post_mlp",
    )(m0, m1, d0, d1, x, att, g, vec)


def ln_stats(t):
    mean = jnp.mean(t, axis=-1, keepdims=True)
    centered = t - mean
    variance = jnp.mean(centered * centered, axis=-1, keepdims=True)
    rstd = lax.rsqrt(variance + LN_EPS)
    return centered * rstd, rstd


def ln_back(xhat, rstd, d):
    return rstd * (d - jnp.mean(d, axis=-1, keepdims=True) - xhat * jnp.mean(d * xhat, axis=-1, keepdims=True))


LN1_ROWS = 400


def ln1_kernel(d0_ref, d1_ref, w_ref, x_ref, res_ref, vec_ref, dx_ref, sum_ref):
    dh = dot_nt(d0_ref[...], w_ref[:, :3 * HALF]) + dot_nt(d1_ref[...], w_ref[:, 3 * HALF:])
    xhat, rstd = ln_stats(x_ref[...].astype(F32))
    dx_ref[...] = (res_ref[...] + ln_back(xhat, rstd, dh * vec_ref[0:1, :])).astype(BF16)

    @pl.when(pl.program_id(0) == 0)
    def _():
        sum_ref[...] = jnp.zeros_like(sum_ref)

    sum_ref[0:1, :] += jnp.sum(dh * xhat, axis=0, keepdims=True)
    sum_ref[1:2, :] += jnp.sum(dh, axis=0, keepdims=True)


def ln1_backward(d0, d1, w_first, x, res, vec):
    rows = pl.BlockSpec((LN1_ROWS, D), lambda i: (i, 0))
    fixed = pl.BlockSpec((8, D), lambda i: (0, 0))
    return pl.pallas_call(
        ln1_kernel,
        grid=(T // LN1_ROWS,),
        in_specs=[pl.BlockSpec((LN1_ROWS, 3 * HALF), lambda i: (i, 0))] * 2
        + [pl.BlockSpec((D, 3 * D), lambda i: (0, 0), pipeline_mode=pl.Buffered(1)), rows, rows, fixed],
        out_specs=[rows, fixed],
        out_shape=[jax.ShapeDtypeStruct((T, D), BF16), jax.ShapeDtypeStruct((8, D), F32)],
        compiler_params=pltpu.CompilerParams(dimension_semantics=("arbitrary",)),
        cost_estimate=pl.CostEstimate(flops=6 * T * D * D, bytes_accessed=30_000_000, transcendentals=T),
        name="ln1_back",
    )(d0, d1, w_first, x, res, vec)


def gather_rows(shard):
    return lax.all_gather(shard, "fsdp", axis=0, tiled=True)


def exchange(val, bit):
    return lax.ppermute(val, "fsdp", [(i, i ^ bit) for i in range(NS)])


def pick(val, axis, index):
    return lax.dynamic_index_in_dim(val, index, axis, keepdims=False)


class Reduction:
    def __init__(self, send, keep, core, x_first, first=0):
        self.rows, self.cols = send.shape[2:]
        self.keep, self.core, self.x_first, self.first = keep, core, x_first, first
        self.near_bit, self.far_bit = (2, 4) if x_first else (4, 2)
        self.got1 = exchange(send, 1)

    def pick_yx(self, near, far):
        return (far, near) if self.x_first else (near, far)

    def term_specs(self, rows, near, far, at):
        def keep_map(s, idx):
            core = idx[2] if self.core else 0
            return (*self.pick_yx(near(s, idx), far(s, idx)), core, self.first // rows + at(s), 0)

        def got_map(s, idx):
            return (*self.pick_yx(near(s, idx), far(s, idx)), at(s), 0)

        return [(self.keep, pl.BlockSpec((None, None, None, rows, self.cols), keep_map)),
                (self.got1, pl.BlockSpec((None, None, rows, self.cols), got_map))]

    def plan(self, stage, n):
        mine = (lambda idx: idx[0], lambda idx: idx[1]) if self.x_first else (lambda idx: idx[1], lambda idx: idx[0])
        my_near, my_far = mine
        if stage == "near":
            per = n // 2
            rows = self.rows // per
            ins = self.term_specs(rows, lambda s, idx: 1 - my_near(idx), lambda s, idx: s // per, lambda s: s % per)
            return ins, (2, self.rows, self.cols), pl.BlockSpec((None, rows, self.cols), lambda s, idx: (s // per, s % per, 0))
        rows = self.rows // n
        far = (lambda s, idx: 1 - my_far(idx)) if stage == "far" else (lambda s, idx: my_far(idx))
        ins = self.term_specs(rows, lambda s, idx: my_near(idx), far, lambda s: s)
        ins.append((self.got2, pl.BlockSpec((None, rows, self.cols), lambda s, idx: (far(s, idx), s, 0))))
        flat = pl.BlockSpec((rows, self.cols), lambda s, idx: (s, 0))
        if stage == "rep":
            ins.append((self.got3, flat))
        return ins, (self.rows, self.cols), flat

    def start(self, stage, value):
        if stage == "near":
            self.got2 = exchange(value, self.near_bit)
        elif stage == "far":
            self.got3 = exchange(value, self.far_bit)
        else:
            self.part = value
            self.got4 = lax.ppermute(value, "rep", [(0, 1), (1, 0)])

    def result(self):
        return self.part + self.got4


def moves_kernel(counts, idx_ref, *refs):
    outs = refs[sum(counts):]
    at = 0
    for count, out in zip(counts, outs):
        total = refs[at][...]
        for ref in refs[at + 1:at + count]:
            total = total + ref[...]
        out[...] = total
        at += count


MOVE_STEPS = 4


def advance(anchor, *moves):
    flat = [(r, stage) for group, stage in moves for r in group]
    plans = [r.plan(stage, MOVE_STEPS) for r, stage in flat]
    me = lax.axis_index("fsdp")
    idx = jnp.stack([lax.rem(me // 2, 2), me // 4, lax.rem(me, 2)]).astype(jnp.int32)
    values = pl.pallas_call(
        functools.partial(moves_kernel, [len(ins) for ins, _, _ in plans]),
        grid_spec=pltpu.PrefetchScalarGridSpec(
            num_scalar_prefetch=1, grid=(MOVE_STEPS,),
            in_specs=[spec for ins, _, _ in plans for _, spec in ins],
            out_specs=[spec for _, _, spec in plans]),
        out_shape=[jax.ShapeDtypeStruct(shape, F32) for _, shape, _ in plans],
        compiler_params=pltpu.CompilerParams(dimension_semantics=("arbitrary",)),
        cost_estimate=pl.CostEstimate(flops=1_000_000_000, bytes_accessed=10_000_000, transcendentals=0),
        name="moves",
    )(idx, *[val for ins, _, _ in plans for val, _ in ins])
    anchor, values = lax.optimization_barrier((anchor, values))
    for (r, stage), value in zip(flat, values):
        r.start(stage, value)
    return anchor


def split_full(full, pieces):
    rows = full.shape[0] // NS
    parts = full.reshape(2, 2, 2, rows, full.shape[1])
    core = lax.rem(lax.axis_index("fsdp"), 2)
    cut = rows // pieces
    return [Reduction(pick(parts[:, :, :, i * cut:(i + 1) * cut], 2, 1 - core), parts, True, i % 2 == 0, i * cut)
            for i in range(pieces)]


def row_major(val):
    return with_layout_constraint(val, Layout(major_to_minor=tuple(range(val.ndim))))


def solution(mesh):
    batch_spec = P(("rep", "fsdp"), None, None)
    row_spec = P("fsdp", None)
    flat_spec = P("fsdp")
    col_spec = P(None, "fsdp")
    param_specs = (row_spec, flat_spec, row_spec, row_spec, flat_spec, row_spec, col_spec)

    def layer_step(x_loc, dz_loc, w_qkv, b_qkv, w_out, w_up, b_up, w_down, vec_params):
        def by_half(val):
            lead = val.shape[:-1]
            return val.reshape(lead + (3, 2, HALF)).swapaxes(-3, -2).reshape(lead + (3 * D,))

        def from_half(val):
            lead = val.shape[:-1]
            return val.reshape(lead + (2, 3, HALF)).swapaxes(-3, -2).reshape(lead + (3 * D,))

        w_first = row_major(jnp.concatenate([by_half(w_qkv.astype(BF16)), w_out.astype(BF16)], axis=1))
        w_first = row_major(gather_rows(w_first))
        wq = w_first[:, :3 * D]
        wo = w_first[:, 3 * D:]
        up_split = w_up.reshape(D // NS, NS, CHUNKS, FC)
        down_split = w_down.reshape(CHUNKS, 2, D // NS, D)
        w_mlp = []
        for c in range(CHUNKS):
            up = up_split[:, :, c].reshape(D // NS, NS * FC).astype(BF16)
            down = jnp.concatenate([down_split[c, 0], down_split[c, 1]], axis=1).astype(BF16)
            shard = row_major(jnp.concatenate([up, down], axis=0))
            w_mlp.append(row_major(lax.all_gather(shard, "fsdp", axis=0, tiled=False)))
        small = jnp.concatenate([b_qkv, b_up, vec_params.reshape(-1)]).astype(BF16)
        small = lax.all_gather(small, "fsdp", axis=0, tiled=False).astype(F32)
        nq, nu = b_qkv.shape[0], b_up.shape[0]
        bias_qkv = by_half(small[:, :nq].reshape(-1))
        bias_up = small[:, nq:nq + nu].reshape(NS, CHUNKS, FC)
        vec = small[:, nq + nu:].reshape(NS, 8, D // NS).transpose(1, 0, 2).reshape(8, D)
        ln1_gain, ln1_bias, out_bias, scale_attn, ln2_gain, ln2_bias, _, scale_mlp = vec

        x_flat = row_major(x_loc.reshape(T, D))
        g_flat = row_major(dz_loc.reshape(T, D))
        x = x_flat.astype(F32)
        d_mlp_bf = row_major((g_flat.astype(F32) * scale_mlp).astype(BF16))
        d_mlp_t = d_mlp_bf.T

        xhat1, _ = ln_stats(x)
        h1 = (xhat1 * ln1_gain + ln1_bias).astype(BF16)
        qkv = (dot(h1, wq) + bias_qkv).astype(BF16)
        heads = attn_forward(qkv)
        att = dot(heads, wo) + out_bias
        y = x + scale_attn * att
        xhat2, _ = ln_stats(y)
        h2 = row_major((xhat2 * ln2_gain + ln2_bias).astype(BF16))
        h2_t = h2.T

        quad = lambda v: v.reshape((2, 2) + v.shape[1:])
        five = lambda v: v.reshape((2, 2, 1) + v.shape[1:])
        partial = []
        grad_bup = []
        mlp = []
        for c in range(CHUNKS):
            m_c, dh_c, up_send, up_keep, down_send, down_keep, gb = mlp_chunk(
                h2, d_mlp_bf, h2_t, d_mlp_t, w_mlp[c], bias_up[:, c].reshape(1, -1))
            mlp.append([Reduction(quad(up_send), five(up_keep), False, True),
                        Reduction(quad(down_send), five(down_keep), False, False)])
            grad_bup.append(gb.reshape(NS, FC))
            partial += [m_c, dh_c]
        partial = advance(partial, (mlp[0], "near"))
        z, g_resid, d_att_bf, vec_sums = post_mlp(partial[0], partial[2], partial[1], partial[3], x_flat, att, g_flat, vec)
        d_heads = dot_nt(d_att_bf, wo).astype(BF16)
        out_red = split_full(dot_tn(heads, d_att_bf), 2)

        d_heads = advance(d_heads, (mlp[0], "far"), (mlp[1], "near"))
        d_qkv0, gb0 = attn_backward(qkv, d_heads, 0)
        qkv0 = split_full(dot_tn(h1, d_qkv0), 2)
        d_qkv0, z = lax.optimization_barrier((d_qkv0, z))
        z = row_major(z.reshape(SEQS, SEQ, D))
        z, d_heads = advance((z, d_heads), (out_red, "near"), (mlp[0], "rep"))
        d_heads = advance(d_heads, (mlp[1], "far"))
        d_qkv1, gb1 = attn_backward(qkv, d_heads, 1)
        gw1 = dot_tn(h1, d_qkv1)
        qkv1 = split_full(gw1, 2)
        d_qkv1 = advance(d_qkv1, (qkv0, "near"), (out_red, "far"), (mlp[1], "rep"))
        d_qkv1 = advance(d_qkv1, (qkv1, "near"))
        dx, ln1_sums = ln1_backward(d_qkv0, d_qkv1, w_first, x_flat, g_resid, vec)
        grad_vec = jnp.concatenate([ln1_sums[:2], vec_sums[2:]], axis=0)
        grad_bqkv = from_half(jnp.sum(jnp.concatenate([gb0, gb1], axis=2), axis=(0, 1))).reshape(NS, nq)
        grad_bup = jnp.stack(grad_bup, axis=1).reshape(NS, nu)
        grad_vec = grad_vec.reshape(8, NS, D // NS).transpose(1, 0, 2).reshape(NS, D)
        small_grads = jnp.concatenate([grad_bqkv, grad_bup, grad_vec, jnp.zeros((NS, 64 * 128 - nq - nu - D), F32)], axis=1)
        small_red = split_full(small_grads.reshape(NS * 64, 128), 1)
        dx = advance(dx, (qkv1, "far"), (qkv0, "far"), (out_red, "rep"))
        dx = row_major(dx.reshape(SEQS, SEQ, D))
        advance((), (qkv1, "rep"), (qkv0, "rep"), (small_red, "near"))
        advance((), (small_red, "far"))
        advance((), (small_red, "rep"))
        whole = lambda group: jnp.concatenate([r.result() for r in group], axis=0)
        grad_w_out = whole(out_red)
        grad_w_qkv = from_half(jnp.concatenate([whole(qkv0), whole(qkv1)], axis=1))
        grad_up = [pair[0].result().reshape(D // NS, NS, FC) for pair in mlp]
        grad_down = [pair[1].result().T for pair in mlp]

        mine = small_red[0].result().reshape(-1)
        return (z, dx, grad_w_qkv, mine[:nq], grad_w_out,
                jnp.stack(grad_up, axis=2).reshape(D // NS, FF), mine[nq:nq + nu],
                jnp.concatenate(grad_down, axis=0), mine[nq + nu:nq + nu + D].reshape(8, D // NS))

    return jax.shard_map(layer_step, mesh=mesh, in_specs=(batch_spec, batch_spec) + param_specs,
                         out_specs=(batch_spec, batch_spec) + param_specs, check_vma=False)
```

profile of v0, /device:TPU:0, one launch (start us, length us, event | category | flops | bytes accessed | tf_op | source)
XLA Modules:
  0.0 704.8 jit_solution(6170894741444562982)
XLA Ops:
  8.3 1.8 copy.63
  11.6 1.9 convert.36
  14.7 5.1 slice_reduce_fusion
  23.1 2.0 maximum_maximum_fusion.2
  25.3 11.7 %all-gather.2 = bf16[8,1,1920]{2,1,0:T(2,128)(2,1)S(1)} all-gather(bf16[1,1,1920]{2,1,0:T(2,128)(2,1)S(1)} %maximum_bitcast_fusion.2), channel_id=1, replica_groups=mesh['rep'=2,'fsdp'=8] {'fsdp'}, dimensions={0}, use_global_device_ids=true | all-gather | bytes 34560 | tf_op jit(solution)/shard_map/all_gather | solution.py:480
  37.0 3.7 copy.61
  40.7 3.2 reshape.199.x_ref
  43.9 6.8 copy.67
  50.7 4.6 reshape.203.g_ref
  55.4 4.6 multiply_convert_fusion.g_ref
  60.0 5.5 copy.69
  68.3 16.4 %add_convert_fusion.q_ref.k_ref.v_ref = bf16[1600,3072]{1,0:T(8,128)(2,1)} fusion(f32[3072]{0:T(1024)S(1)} %add.111, bf16[1024,4096]{1,0:T(8,128)(2,1)} %all-gather.7.cloned.1.call-done.w_ref, bf16[1600,1024]{1,0:T(8,128)(2,1)S(1)} %reshape.199.x_ref, f32[1024]{0:T(1024)S(1)} %bitcast.213, f32[1024]{0:T(1024)S(1)} %bitcast.216, f32[1600]{0:T(1024)S(1)} %add_rsqrt_fusion.1, ...), kind=kOutput, calls=%fused_computation | convolution fusion | flops 10085990400 | bytes 19431936 | tf_op jit(solution)/shard_map/dot_general | solution.py:38
  84.7 20.8 %attn_fwd.1 = bf16[1600,1024]{1,0:T(8,128)(2,1)} custom-call(bf16[1600,3072]{1,0:T(8,128)(2,1)} %add_convert_fusion.q_ref.k_ref.v_ref, bf16[1600,3072]{1,0:T(8,128)(2,1)} %add_convert_fusion.q_ref.k_ref.v_ref, bf16[1600,3072]{1,0:T(8,128)(2,1)} %add_convert_fusion.q_ref.k_ref.v_ref), custom_call_target="tpu_custom_call" | custom-call | flops 8000000000 | bytes 13000000 | tf_op jit(solution)/shard_map/attn_fwd/pallas_call | solution.py:156
  105.5 7.0 fusion.9
  115.3 3.1 add_convert_fusion.1.h_ref
  118.4 5.4 copy.68
  123.8 72.8 %mlp_fwd_bwd.2 = (f32[1600,1024]{1,0:T(8,128)}, f32[1600,1024]{1,0:T(8,128)}, f32[4,128,2048]{2,1,0:T(8,128)}, f32[4,128,2048]{2,1,0:T(8,128)}, f32[4,1024,256]{...) custom-call(bf16[1600,1024]{1,0:T(8,128)(2,1)} %add_convert_fusion.1.h_ref, ...), custom_call_target="tpu_custom_call" | custom-call | flops 40265318400 | bytes 60000000 | tf_op jit(solution)/shard_map/mlp_fwd_bwd/pallas_call | solution.py:233
  197.2 72.1 %mlp_fwd_bwd.3 = (f32[1600,1024]{1,0:T(8,128)}, f32[1600,1024]{1,0:T(8,128)}, f32[4,128,2048]{2,1,0:T(8,128)}, f32[4,128,2048]{2,1,0:T(8,128)}, f32[4,1024,256]{...) custom-call(bf16[1600,1024]{1,0:T(8,128)(2,1)} %add_convert_fusion.1.h_ref, ...), custom_call_target="tpu_custom_call" | custom-call | flops 40265318400 | bytes 60000000 | tf_op jit(solution)/shard_map/mlp_fwd_bwd/pallas_call | solution.py:233
  270.5 6.4 moves.10
  279.6 19.9 %post_mlp.1 = (bf16[1600,1024]{1,0:T(8,128)(2,1)}, f32[1600,1024]{1,0:T(8,128)}, bf16[1600,1024]{1,0:T(8,128)(2,1)}, f32[8,1024]{1,0:T(8,128)}) custom-call(f32[1600,1024]{1,0:T(8,128)} %get-tuple-element.113.m0_ref, f32[1600,1024]{1,0:T(8,128)} %get-tuple-element.114.m1_ref, f32[1600,1024]{1,0:T(8,128)} %get-tuple-element.115.d0_ref, ...), custom_call_target="tpu_custom_call" | custom-call | flops 5000000000 | bytes 56000000 | tf_op jit(solution)/shard_map/post_mlp/pallas_call | solution.py:282
  299.6 6.9 fusion.19
  311.2 6.5 convolution_convert_fusion.g_ref
  317.7 7.2 %collective-permute-done.2.refs_2_.refs_6_ = f32[2,128,2048]{2,1,0:T(8,128)S(1)} collective-permute-done((f32[2,128,2048]{2,1,0:T(8,128)}, f32[2,128,2048]{2,1,0:T(8,128)S(1)}, u32[]{:S(2)}, u32[]{:S(2)}) %collective-permute-start.2) | collective-permute-done | bytes 2097184 | tf_op jit(solution)/shard_map/ppermute | solution.py:344
  326.3 9.0 %moves.11 = (f32[128,2048]{1,0:T(8,128)}, f32[1024,256]{1,0:T(8,128)}, f32[2,128,2048]{2,1,0:T(8,128)}, f32[2,1024,256]{2,1,0:T(8,128)}) custom-call(s32[3]{0:T(128)} %pad_add_fusion.idx_ref, f32[2,2,1,128,2048]{4,3,2,1,0:T(8,128)} %bitcast.157, f32[2,2,128,2048]{3,2,1,0:T(8,128)} %collective-permute-done.refs_1_.refs_5_, f32[2,128,2048]{2,1,0:T(8,128)} %copy-done.7, ...), custom_call_target="tpu_custom_call" | custom-call | flops 1000000000 | bytes 10000000 | tf_op jit(solution)/shard_map/moves/pallas_call | solution.py:421
  335.3 33.6 %attn_bwd.2 = (bf16[1600,1536]{1,0:T(8,128)(2,1)}, f32[4,1,1536]{2,1,0:T(1,128)}) custom-call(bf16[1600,3072]{1,0:T(8,128)(2,1)} %add_convert_fusion.q_ref.k_ref.v_ref, bf16[1600,3072]{1,0:T(8,128)(2,1)} %add_convert_fusion.q_ref.k_ref.v_ref, bf16[1600,3072]{1,0:T(8,128)(2,1)} %add_convert_fusion.q_ref.k_ref.v_ref, ...), custom_call_target="tpu_custom_call" | custom-call | flops 16000000000 | bytes 12000000 | tf_op jit(solution)/shard_map/attn_bwd/pallas_call | solution.py:170
  371.9 10.5 %fusion.12 = f32[1024,1536]{1,0:T(8,128)} fusion(bf16[1600,1536]{1,0:T(8,128)(2,1)} %get-tuple-element.139.d0_ref, bf16[1600,1024]{1,0:T(8,128)(2,1)S(1)} %copy-done.3, f32[1024]{0:T(1024)S(1)} %bitcast.214, f32[1024]{0:T(1024)S(1)} %bitcast.217, f32[1600]{0:T(1024)S(1)} %copy-done.36, f32[1600]{0:T(1024)S(1)} %copy-done.29), kind=kOutput, calls=%fused_computation.63 | convolution fusion | flops 5042995200 | bytes 14504448 | tf_op jit(solution)/shard_map/dot_general | solution.py:46
  382.4 4.7 reshape.216
  388.3 3.3 fusion.16
  394.1 45.9 %collective-permute-done.8.refs_7_ = f32[128,2048]{1,0:T(8,128)} collective-permute-done((f32[128,2048]{1,0:T(8,128)}, f32[128,2048]{1,0:T(8,128)}, u32[]{:S(2)}, u32[]{:S(2)}) %collective-permute-start.8) | collective-permute-done | bytes 1048608 | tf_op jit(solution)/shard_map/ppermute | solution.py:344
  440.1 6.8 moves.12
  449.1 5.3 moves.13
  454.4 33.7 %attn_bwd.3 = (bf16[1600,1536]{1,0:T(8,128)(2,1)}, f32[4,1,1536]{2,1,0:T(1,128)}) custom-call(bf16[1600,3072]{1,0:T(8,128)(2,1)} %add_convert_fusion.q_ref.k_ref.v_ref, bf16[1600,3072]{1,0:T(8,128)(2,1)} %add_convert_fusion.q_ref.k_ref.v_ref, bf16[1600,3072]{1,0:T(8,128)(2,1)} %add_convert_fusion.q_ref.k_ref.v_ref, ...), custom_call_target="tpu_custom_call" | custom-call | flops 16000000000 | bytes 12000000 | tf_op jit(solution)/shard_map/attn_bwd/pallas_call | solution.py:170
  488.4 9.0 %fusion.10 = f32[1024,1536]{1,0:T(8,128)S(1)} fusion(bf16[1600,1536]{1,0:T(8,128)(2,1)} %get-tuple-element.160.d1_ref, bf16[1600,1024]{1,0:T(8,128)(2,1)S(1)} %copy-done.3, f32[1024]{0:T(1024)S(1)} %bitcast.215, f32[1024]{0:T(1024)S(1)} %bitcast.218, f32[1600]{0:T(1024)S(1)} %copy-done.36, f32[1600]{0:T(1024)S(1)} %copy-done.29), kind=kOutput, calls=%fused_computation.62 | convolution fusion | flops 5042995200 | bytes 14504448 | tf_op jit(solution)/shard_map/dot_general | solution.py:46
  498.0 2.0 copy-done
  504.5 1.7 collective-permute-start.40
  506.2 7.2 %collective-permute-done.16.refs_13_ = f32[128,2048]{1,0:T(8,128)} collective-permute-done((f32[128,2048]{1,0:T(8,128)}, f32[128,2048]{1,0:T(8,128)}, u32[]{:S(2)}, u32[]{:S(2)}) %collective-permute-start.16) | collective-permute-done | bytes 1048608 | tf_op jit(solution)/shard_map/ppermute | solution.py:344
  514.9 11.1 %collective-permute-done.17.refs_17_ = f32[1024,256]{1,0:T(8,128)} collective-permute-done((f32[1024,256]{1,0:T(8,128)S(1)}, f32[1024,256]{1,0:T(8,128)}, u32[]{:S(2)}, u32[]{:S(2)}) %collective-permute-start.17) | collective-permute-done | bytes 1048608 | tf_op jit(solution)/shard_map/ppermute | solution.py:344
  526.0 8.0 %moves.14 = (f32[2,64,1536]{2,1,0:T(8,128)}, f32[2,64,1536]{2,1,0:T(8,128)}, f32[64,1024]{1,0:T(8,128)}, f32[64,1024]{1,0:T(8,128)}, f32[128,2048]{1,0:T(8,128)}, /*index=5*/f32[1024,256]{1,0:T(8,128)}) custom-call(s32[3]{0:T(128)} %pad_add_fusion.idx_ref, f32[2,2,2,128,1536]{4,3,2,1,0:T(8,128)} %bitcast.136, ...), custom_call_target="tpu_custom_call" | custom-call | flops 1000000000 | bytes 10000000 | tf_op jit(solution)/shard_map/moves/pallas_call | solution.py:421
  535.7 5.6 copy.76
  546.0 6.5 collective-permute-done.42
  553.0 2.8 add_bitcast_fusion.1
  559.0 4.7 moves.15
  566.8 19.7 %ln1_back.1 = (bf16[1600,1024]{1,0:T(8,128)(2,1)}, f32[8,1024]{1,0:T(8,128)}) custom-call(bf16[1600,1536]{1,0:T(8,128)(2,1)} %get-tuple-element.139.d0_ref, bf16[1600,1536]{1,0:T(8,128)(2,1)} %get-tuple-element.160.d1_ref, bf16[1024,4096]{1,0:T(8,128)(2,1)} %all-gather.7.cloned.1.call-done.w_ref, bf16[1600,1024]{1,0:T(8,128)(2,1)} %copy-done.2, ...), custom_call_target="tpu_custom_call" | custom-call | flops 10066329600 | bytes 30000000 | tf_op jit(solution)/shard_map/ln1_back/pallas_call | solution.py:326
  587.5 3.7 collective-permute-done.21.refs_5_.refs_6_
  592.1 5.5 moves.16
  597.6 1.7 collective-permute-start.26
  601.7 2.2 collective-permute-done.43
  603.9 2.4 add_bitcast_fusion
  606.3 1.7 add.131
  611.5 3.9 collective-permute-done.28.refs_11_
  617.7 5.4 moves.17
  624.5 1.8 pad_maximum_fusion
  628.3 3.3 moves.18
  632.6 2.8 pad_maximum_fusion.1
  635.4 3.0 copy.75
  638.4 4.0 reshape.227
  642.5 1.8 copy.79
  644.3 4.9 reshape.220
  649.2 5.5 copy.77
  657.5 3.4 moves.19
  669.9 5.4 collective-permute-done.34
  675.3 8.4 %collective-permute-done.33 = f32[64,1536]{1,0:T(8,128)S(1)} collective-permute-done((f32[64,1536]{1,0:T(8,128)S(1)}, f32[64,1536]{1,0:T(8,128)S(1)}, u32[]{:S(2)}, u32[]{:S(2)}) %collective-permute-start.33) | collective-permute-done | bytes 393248 | tf_op jit(solution)/shard_map/ppermute | solution.py:396
  683.8 7.7 %collective-permute-done.32 = f32[64,1536]{1,0:T(8,128)S(1)} collective-permute-done((f32[64,1536]{1,0:T(8,128)S(1)}, f32[64,1536]{1,0:T(8,128)S(1)}, u32[]{:S(2)}, u32[]{:S(2)}) %collective-permute-start.32) | collective-permute-done | bytes 393248 | tf_op jit(solution)/shard_map/ppermute | solution.py:396
  691.5 4.2 collective-permute-done.31
  (257 shorter events, 81.1 us)
Async XLA Ops:
  7.2 61.0 %all-gather.7.cloned.1.call-start = ((), (), s32[]{:S(2)}) async-start(), calls=%async_computation | async-start | bytes 9437184 | tf_op jit(solution)/shard_map/all_gather | solution.py:340
  11.5 112.3 %all-gather.9.cloned.1.call-start = ((), (), s32[]{:S(2)}) async-start(), calls=%async_computation.1 | async-start | bytes 9437184 | tf_op jit(solution)/shard_map/all_gather | solution.py:478
  21.7 15.3 %copy-start.10 = (bf16[32,50,1024]{2,0,1:T(8,128)(2,1)S(1)}, bf16[32,50,1024]{2,0,1:T(8,128)(2,1)}, u32[]{:S(2)}) copy-start(bf16[32,50,1024]{2,0,1:T(8,128)(2,1)} %param.9) | copy-start | bytes 9830404
  21.8 175.4 %all-gather.11.cloned.1.call-start = ((), (), s32[]{:S(2)}) async-start(), calls=%async_computation.2 | async-start | bytes 9437184 | tf_op jit(solution)/shard_map/all_gather | solution.py:478
  43.9 70.2 %copy-start.2 = (bf16[1600,1024]{1,0:T(8,128)(2,1)}, bf16[1600,1024]{1,0:T(8,128)(2,1)S(1)}, u32[]{:S(2)}) copy-start(bf16[1600,1024]{1,0:T(8,128)(2,1)S(1)} %reshape.199.x_ref) | copy-start | bytes 9830404
  55.3 12.9 %copy-start.37 = (f32[1,8,128]{2,0,1:T(1,128)}, f32[1,8,128]{2,0,1:T(1,128)S(1)}, u32[]{:S(2)}) copy-start(f32[1,8,128]{2,0,1:T(1,128)S(1)} %get-tuple-element.252) | copy-start | bytes 12292
  55.3 12.9 %copy-start.39 = (f32[1,8,128]{2,0,1:T(1,128)}, f32[1,8,128]{2,0,1:T(1,128)S(1)}, u32[]{:S(2)}) copy-start(f32[1,8,128]{2,0,1:T(1,128)S(1)} %get-tuple-element.253) | copy-start | bytes 12292
  67.2 17.5 %copy-start.28 = (f32[1600]{0:T(1024)}, f32[1600]{0:T(1024)S(1)}, u32[]{:S(2)}) copy-start(f32[1600]{0:T(1024)S(1)} %broadcast_multiply_fusion.1) | copy-start | bytes 19204
  68.2 16.5 %copy-start.35 = (f32[1600]{0:T(1024)}, f32[1600]{0:T(1024)S(1)}, u32[]{:S(2)}) copy-start(f32[1600]{0:T(1024)S(1)} %add_rsqrt_fusion.1) | copy-start | bytes 19204
  196.7 73.8 %collective-permute-start = (f32[2,2,128,2048]{3,2,1,0:T(8,128)}, f32[2,2,128,2048]{3,2,1,0:T(8,128)}, u32[]{:S(2)}, u32[]{:S(2)}) collective-permute-start(f32[2,2,128,2048]{3,2,1,0:T(8,128)} %bitcast.227), channel_id=1, source_target_pairs={{0,1},{1,0},{2,3},{3,2},{4,5},{5,4},{6,7},{7,6},{8,9},{9,8},{10,11... | collective-permute-start | bytes 12582920 | tf_op jit(solution)/shard_map/ppermute | solution.py:344
  197.0 73.5 %collective-permute-start.1 = (f32[2,2,1024,256]{3,2,1,0:T(8,128)}, f32[2,2,1024,256]{3,2,1,0:T(8,128)}, u32[]{:S(2)}, u32[]{:S(2)}) collective-permute-start(f32[2,2,1024,256]{3,2,1,0:T(8,128)} %bitcast.226), channel_id=1, source_target_pairs={{0,1},{1,0},{2,3},{3,2},{4,5},{5,4},{6,7},{7,6},{8,9},{9,8},{10,11... | collective-permute-start | bytes 12582920 | tf_op jit(solution)/shard_map/ppermute | solution.py:344
  269.3 48.4 %collective-permute-start.4 = (f32[2,2,128,2048]{3,2,1,0:T(8,128)}, f32[2,2,128,2048]{3,2,1,0:T(8,128)}, u32[]{:S(2)}, u32[]{:S(2)}) collective-permute-start(f32[2,2,128,2048]{3,2,1,0:T(8,128)} %bitcast.225), channel_id=1, source_target_pairs={{0,1},{1,0},{2,3},{3,2},{4,5},{5,4},{6,7},{7,6},{8,9},{9,8},{10,11... | collective-permute-start | bytes 12582920 | tf_op jit(solution)/shard_map/ppermute | solution.py:344
  269.6 48.1 %collective-permute-start.5 = (f32[2,2,1024,256]{3,2,1,0:T(8,128)}, f32[2,2,1024,256]{3,2,1,0:T(8,128)}, u32[]{:S(2)}, u32[]{:S(2)}) collective-permute-start(f32[2,2,1024,256]{3,2,1,0:T(8,128)} %bitcast.224), channel_id=1, source_target_pairs={{0,1},{1,0},{2,3},{3,2},{4,5},{5,4},{6,7},{7,6},{8,9},{9,8},{10,11... | collective-permute-start | bytes 12582920 | tf_op jit(solution)/shard_map/ppermute | solution.py:344
  276.9 48.1 %collective-permute-start.2 = (f32[2,128,2048]{2,1,0:T(8,128)}, f32[2,128,2048]{2,1,0:T(8,128)S(1)}, u32[]{:S(2)}, u32[]{:S(2)}) collective-permute-start(f32[2,128,2048]{2,1,0:T(8,128)} %get-tuple-element.118), channel_id=1, source_target_pairs={{0,2},{1,3},{2,0},{3,1},{4,6},{5,7},{6,4},{7,5},{8,10},{9,11},{10,... | collective-permute-start | bytes 6291464 | tf_op jit(solution)/shard_map/ppermute | solution.py:344
  278.4 47.9 %collective-permute-start.3 = (f32[2,1024,256]{2,1,0:T(8,128)}, f32[2,1024,256]{2,1,0:T(8,128)}, u32[]{:S(2)}, u32[]{:S(2)}) collective-permute-start(f32[2,1024,256]{2,1,0:T(8,128)} %get-tuple-element.119), channel_id=1, source_target_pairs={{0,4},{1,5},{2,6},{3,7},{4,0},{5,1},{6,2},{7,3},{8,12},{9,13},{10,... | collective-permute-start | bytes 6291464 | tf_op jit(solution)/shard_map/ppermute | solution.py:344
  309.5 78.2 %collective-permute-start.6 = (f32[2,2,64,1024]{3,2,1,0:T(8,128)}, f32[2,2,64,1024]{3,2,1,0:T(8,128)}, u32[]{:S(2)}, u32[]{:S(2)}) collective-permute-start(f32[2,2,64,1024]{3,2,1,0:T(8,128)} %dynamic-slice_bitcast_fusion.5), channel_id=1, source_target_pairs={{0,1},{1,0},{2,3},{3,2},{4,5},{5,4},{6,7},{7,6},{8,9},{9,8},{10,11... | collective-permute-start | bytes 3145736 | tf_op jit(solution)/shard_map/ppermute | solution.py:344
  317.7 76.4 %collective-permute-start.7 = (f32[2,2,64,1024]{3,2,1,0:T(8,128)}, f32[2,2,64,1024]{3,2,1,0:T(8,128)}, u32[]{:S(2)}, u32[]{:S(2)}) collective-permute-start(f32[2,2,64,1024]{3,2,1,0:T(8,128)} %dynamic-slice_bitcast_fusion.4), channel_id=1, source_target_pairs={{0,1},{1,0},{2,3},{3,2},{4,5},{5,4},{6,7},{7,6},{8,9},{9,8},{10,11... | collective-permute-start | bytes 3145736 | tf_op jit(solution)/shard_map/ppermute | solution.py:344
  335.3 36.6 %copy-start.3 = (bf16[1600,1024]{1,0:T(8,128)(2,1)S(1)}, bf16[1600,1024]{1,0:T(8,128)(2,1)}, u32[]{:S(2)}) copy-start(bf16[1600,1024]{1,0:T(8,128)(2,1)} %copy-done.2) | copy-start | bytes 9830404
  335.3 36.6 %copy-start.29 = (f32[1600]{0:T(1024)S(1)}, f32[1600]{0:T(1024)}, u32[]{:S(2)}) copy-start(f32[1600]{0:T(1024)} %copy-done.28) | copy-start | bytes 19204
  335.3 36.5 %copy-start.36 = (f32[1600]{0:T(1024)S(1)}, f32[1600]{0:T(1024)}, u32[]{:S(2)}) copy-start(f32[1600]{0:T(1024)} %copy-done.35) | copy-start | bytes 19204
  335.3 36.5 %copy-start.38 = (f32[1,8,128]{2,0,1:T(1,128)S(1)}, f32[1,8,128]{2,0,1:T(1,128)}, u32[]{:S(2)}) copy-start(f32[1,8,128]{2,0,1:T(1,128)} %copy-done.37) | copy-start | bytes 12292
  335.3 36.5 %copy-start.40 = (f32[1,8,128]{2,0,1:T(1,128)S(1)}, f32[1,8,128]{2,0,1:T(1,128)}, u32[]{:S(2)}) copy-start(f32[1,8,128]{2,0,1:T(1,128)} %copy-done.39) | copy-start | bytes 12292
  369.0 78.4 %collective-permute-start.10 = (f32[2,128,2048]{2,1,0:T(8,128)}, f32[2,128,2048]{2,1,0:T(8,128)}, u32[]{:S(2)}, u32[]{:S(2)}) collective-permute-start(f32[2,128,2048]{2,1,0:T(8,128)} %get-tuple-element.141), channel_id=1, source_target_pairs={{0,2},{1,3},{2,0},{3,1},{4,6},{5,7},{6,4},{7,5},{8,10},{9,11},{10,... | collective-permute-start | bytes 6291464 | tf_op jit(solution)/shard_map/ppermute | solution.py:344
  370.5 78.6 %collective-permute-start.11 = (f32[2,1024,256]{2,1,0:T(8,128)}, f32[2,1024,256]{2,1,0:T(8,128)}, u32[]{:S(2)}, u32[]{:S(2)}) collective-permute-start(f32[2,1024,256]{2,1,0:T(8,128)} %get-tuple-element.142), channel_id=1, source_target_pairs={{0,4},{1,5},{2,6},{3,7},{4,0},{5,1},{6,2},{7,3},{8,12},{9,13},{10,... | collective-permute-start | bytes 6291464 | tf_op jit(solution)/shard_map/ppermute | solution.py:344
  387.1 53.0 %collective-permute-start.8 = (f32[128,2048]{1,0:T(8,128)}, f32[128,2048]{1,0:T(8,128)}, u32[]{:S(2)}, u32[]{:S(2)}) collective-permute-start(f32[128,2048]{1,0:T(8,128)} %get-tuple-element.132), channel_id=1, source_target_pairs={{0,4},{1,5},{2,6},{3,7},{4,0},{5,1},{6,2},{7,3},{8,12},{9,13},{10,... | collective-permute-start | bytes 3145736 | tf_op jit(solution)/shard_map/ppermute | solution.py:344
  387.7 52.3 %collective-permute-start.9 = (f32[1024,256]{1,0:T(8,128)}, f32[1024,256]{1,0:T(8,128)}, u32[]{:S(2)}, u32[]{:S(2)}) collective-permute-start(f32[1024,256]{1,0:T(8,128)} %get-tuple-element.133), channel_id=1, source_target_pairs={{0,2},{1,3},{2,0},{3,1},{4,6},{5,7},{6,4},{7,5},{8,10},{9,11},{10,... | collective-permute-start | bytes 3145736 | tf_op jit(solution)/shard_map/ppermute | solution.py:344
  394.1 107.1 %collective-permute-start.12 = (f32[2,2,64,1536]{3,2,1,0:T(8,128)}, f32[2,2,64,1536]{3,2,1,0:T(8,128)}, u32[]{:S(2)}, u32[]{:S(2)}) collective-permute-start(f32[2,2,64,1536]{3,2,1,0:T(8,128)} %dynamic-slice_bitcast_fusion.3), channel_id=1, source_target_pairs={{0,1},{1,0},{2,3},{3,2},{4,5},{5,4},{6,7},{7,6},{8,9},{9,8},{10,11... | collective-permute-start | bytes 4718600 | tf_op jit(solution)/shard_map/ppermute | solution.py:344
  440.0 62.7 %collective-permute-start.13 = (f32[2,2,64,1536]{3,2,1,0:T(8,128)}, f32[2,2,64,1536]{3,2,1,0:T(8,128)}, u32[]{:S(2)}, u32[]{:S(2)}) collective-permute-start(f32[2,2,64,1536]{3,2,1,0:T(8,128)} %dynamic-slice_bitcast_fusion.2), channel_id=1, source_target_pairs={{0,1},{1,0},{2,3},{3,2},{4,5},{5,4},{6,7},{7,6},{8,9},{9,8},{10,11... | collective-permute-start | bytes 4718600 | tf_op jit(solution)/shard_map/ppermute | solution.py:344
  446.8 57.1 %collective-permute-start.14 = (f32[2,64,1024]{2,1,0:T(8,128)}, f32[2,64,1024]{2,1,0:T(8,128)}, u32[]{:S(2)}, u32[]{:S(2)}) collective-permute-start(f32[2,64,1024]{2,1,0:T(8,128)} %get-tuple-element.147), channel_id=1, source_target_pairs={{0,2},{1,3},{2,0},{3,1},{4,6},{5,7},{6,4},{7,5},{8,10},{9,11},{10,... | collective-permute-start | bytes 1572872 | tf_op jit(solution)/shard_map/ppermute | solution.py:344
  447.4 57.1 %collective-permute-start.15 = (f32[2,64,1024]{2,1,0:T(8,128)}, f32[2,64,1024]{2,1,0:T(8,128)}, u32[]{:S(2)}, u32[]{:S(2)}) collective-permute-start(f32[2,64,1024]{2,1,0:T(8,128)} %get-tuple-element.148), channel_id=1, source_target_pairs={{0,4},{1,5},{2,6},{3,7},{4,0},{5,1},{6,2},{7,3},{8,12},{9,13},{10,... | collective-permute-start | bytes 1572872 | tf_op jit(solution)/shard_map/ppermute | solution.py:344
  488.1 25.3 %collective-permute-start.16 = (f32[128,2048]{1,0:T(8,128)}, f32[128,2048]{1,0:T(8,128)}, u32[]{:S(2)}, u32[]{:S(2)}) collective-permute-start(f32[128,2048]{1,0:T(8,128)} %get-tuple-element.149), channel_id=1, source_target_pairs={{0,4},{1,5},{2,6},{3,7},{4,0},{5,1},{6,2},{7,3},{8,12},{9,13},{10,... | collective-permute-start | bytes 3145736 | tf_op jit(solution)/shard_map/ppermute | solution.py:344
  501.2 24.8 %collective-permute-start.17 = (f32[1024,256]{1,0:T(8,128)S(1)}, f32[1024,256]{1,0:T(8,128)}, u32[]{:S(2)}, u32[]{:S(2)}) collective-permute-start(f32[1024,256]{1,0:T(8,128)S(1)} %copy-done.45), channel_id=1, source_target_pairs={{0,2},{1,3},{2,0},{3,1},{4,6},{5,7},{6,4},{7,5},{8,10},{9,11},{10,... | collective-permute-start | bytes 3145736 | tf_op jit(solution)/shard_map/ppermute | solution.py:344
  502.7 53.0 %collective-permute-start.18 = (f32[2,2,64,1536]{3,2,1,0:T(8,128)}, f32[2,2,64,1536]{3,2,1,0:T(8,128)S(1)}, u32[]{:S(2)}, u32[]{:S(2)}) collective-permute-start(f32[2,2,64,1536]{3,2,1,0:T(8,128)} %dynamic-slice_bitcast_fusion.1), channel_id=1, source_target_pairs={{0,1},{1,0},{2,3},{3,2},{4,5},{5,4},{6,7},{7,6},{8,9},{9,8},{10,11... | collective-permute-start | bytes 4718600 | tf_op jit(solution)/shard_map/ppermute | solution.py:344
  504.0 31.6 %copy-start.34 = (f32[1,2048]{1,0:T(1,128)S(1)}, f32[1,2048]{1,0:T(1,128)}, u32[]{:S(2)}) copy-start(f32[1,2048]{1,0:T(1,128)} %get-tuple-element.183) | copy-start | bytes 24580
  504.0 31.7 %copy-start.33 = (f32[1,2048]{1,0:T(1,128)S(1)}, f32[1,2048]{1,0:T(1,128)}, u32[]{:S(2)}) copy-start(f32[1,2048]{1,0:T(1,128)} %get-tuple-element.182) | copy-start | bytes 24580
  504.0 31.7 %copy-start.30 = (f32[8,1024]{1,0:T(8,128)S(1)}, f32[8,1024]{1,0:T(8,128)}, u32[]{:S(2)}) copy-start(f32[8,1024]{1,0:T(8,128)} %get-tuple-element.185) | copy-start | bytes 98308
  504.0 53.4 %collective-permute-start.19 = (f32[2,2,64,1536]{3,2,1,0:T(8,128)}, f32[2,2,64,1536]{3,2,1,0:T(8,128)S(1)}, u32[]{:S(2)}, u32[]{:S(2)}) collective-permute-start(f32[2,2,64,1536]{3,2,1,0:T(8,128)} %dynamic-slice_bitcast_fusion), channel_id=1, source_target_pairs={{0,1},{1,0},{2,3},{3,2},{4,5},{5,4},{6,7},{7,6},{8,9},{9,8},{10,11... | collective-permute-start | bytes 4718600 | tf_op jit(solution)/shard_map/ppermute | solution.py:344
  504.5 36.9 %collective-permute-start.40 = (f32[128,2048]{1,0:T(8,128)}, f32[128,2048]{1,0:T(8,128)}, u32[]{:S(2)}, u32[]{:S(2)}) collective-permute-start(f32[128,2048]{1,0:T(8,128)} %get-tuple-element.193), channel_id=1, source_target_pairs={{0,8},{8,0},{1,9},{9,1},{2,10},{10,2},{3,11},{11,3},{4,12},{12,4},... | collective-permute-start | bytes 3145736 | tf_op jit(solution)/shard_map/ppermute | solution.py:396
  513.4 39.0 %collective-permute-start.42 = (f32[1024,256]{1,0:T(8,128)}, f32[1024,256]{1,0:T(8,128)}, u32[]{:S(2)}, u32[]{:S(2)}) collective-permute-start(f32[1024,256]{1,0:T(8,128)} %get-tuple-element.195), channel_id=1, source_target_pairs={{0,8},{8,0},{1,9},{9,1},{2,10},{10,2},{3,11},{11,3},{4,12},{12,4},... | collective-permute-start | bytes 3145736 | tf_op jit(solution)/shard_map/ppermute | solution.py:396
  534.1 32.2 %collective-permute-start.22 = (f32[2,64,1536]{2,1,0:T(8,128)}, f32[2,64,1536]{2,1,0:T(8,128)}, u32[]{:S(2)}, u32[]{:S(2)}) collective-permute-start(f32[2,64,1536]{2,1,0:T(8,128)} %get-tuple-element.165), channel_id=1, source_target_pairs={{0,2},{1,3},{2,0},{3,1},{4,6},{5,7},{6,4},{7,5},{8,10},{9,11},{10,... | collective-permute-start | bytes 2359304 | tf_op jit(solution)/shard_map/ppermute | solution.py:344
  544.4 19.3 %collective-permute-start.24 = (f32[64,1024]{1,0:T(8,128)}, f32[64,1024]{1,0:T(8,128)S(1)}, u32[]{:S(2)}, u32[]{:S(2)}) collective-permute-start(f32[64,1024]{1,0:T(8,128)} %get-tuple-element.167), channel_id=1, source_target_pairs={{0,4},{1,5},{2,6},{3,7},{4,0},{5,1},{6,2},{7,3},{8,12},{9,13},{10,... | collective-permute-start | bytes 786440 | tf_op jit(solution)/shard_map/ppermute | solution.py:344
  552.4 12.4 %collective-permute-start.25 = (f32[64,1024]{1,0:T(8,128)}, f32[64,1024]{1,0:T(8,128)}, u32[]{:S(2)}, u32[]{:S(2)}) collective-permute-start(f32[64,1024]{1,0:T(8,128)} %get-tuple-element.168), channel_id=1, source_target_pairs={{0,2},{1,3},{2,0},{3,1},{4,6},{5,7},{6,4},{7,5},{8,10},{9,11},{10,... | collective-permute-start | bytes 786440 | tf_op jit(solution)/shard_map/ppermute | solution.py:344
  555.7 31.7 %collective-permute-start.23 = (f32[2,64,1536]{2,1,0:T(8,128)}, f32[2,64,1536]{2,1,0:T(8,128)}, u32[]{:S(2)}, u32[]{:S(2)}) collective-permute-start(f32[2,64,1536]{2,1,0:T(8,128)} %get-tuple-element.166), channel_id=1, source_target_pairs={{0,4},{1,5},{2,6},{3,7},{4,0},{5,1},{6,2},{7,3},{8,12},{9,13},{10,... | collective-permute-start | bytes 2359304 | tf_op jit(solution)/shard_map/ppermute | solution.py:344
  557.4 43.8 %collective-permute-start.41 = (f32[128,2048]{1,0:T(8,128)}, f32[128,2048]{1,0:T(8,128)}, u32[]{:S(2)}, u32[]{:S(2)}) collective-permute-start(f32[128,2048]{1,0:T(8,128)} %get-tuple-element.194), channel_id=1, source_target_pairs={{0,8},{8,0},{1,9},{9,1},{2,10},{10,2},{3,11},{11,3},{4,12},{12,4},... | collective-permute-start | bytes 3145736 | tf_op jit(solution)/shard_map/ppermute | solution.py:396
  563.6 22.9 %copy-start.25 = (f32[64,1024]{1,0:T(8,128)}, f32[64,1024]{1,0:T(8,128)S(1)}, u32[]{:S(2)}) copy-start(f32[64,1024]{1,0:T(8,128)S(1)} %collective-permute-done.24.refs_15_) | copy-start | bytes 786436
  563.6 40.2 %collective-permute-start.43 = (f32[1024,256]{1,0:T(8,128)}, f32[1024,256]{1,0:T(8,128)}, u32[]{:S(2)}, u32[]{:S(2)}) collective-permute-start(f32[1024,256]{1,0:T(8,128)} %get-tuple-element.196), channel_id=1, source_target_pairs={{0,8},{8,0},{1,9},{9,1},{2,10},{10,2},{3,11},{11,3},{4,12},{12,4},... | collective-permute-start | bytes 3145736 | tf_op jit(solution)/shard_map/ppermute | solution.py:396
  564.8 22.6 %collective-permute-start.20 = (f32[2,64,1536]{2,1,0:T(8,128)}, f32[2,64,1536]{2,1,0:T(8,128)S(1)}, u32[]{:S(2)}, u32[]{:S(2)}) collective-permute-start(f32[2,64,1536]{2,1,0:T(8,128)} %get-tuple-element.163), channel_id=1, source_target_pairs={{0,2},{1,3},{2,0},{3,1},{4,6},{5,7},{6,4},{7,5},{8,10},{9,11},{10,... | collective-permute-start | bytes 2359304 | tf_op jit(solution)/shard_map/ppermute | solution.py:344
  566.2 24.9 %collective-permute-start.21 = (f32[2,64,1536]{2,1,0:T(8,128)}, f32[2,64,1536]{2,1,0:T(8,128)S(1)}, u32[]{:S(2)}, u32[]{:S(2)}) collective-permute-start(f32[2,64,1536]{2,1,0:T(8,128)} %get-tuple-element.164), channel_id=1, source_target_pairs={{0,4},{1,5},{2,6},{3,7},{4,0},{5,1},{6,2},{7,3},{8,12},{9,13},{10,... | collective-permute-start | bytes 2359304 | tf_op jit(solution)/shard_map/ppermute | solution.py:344
  587.4 14.3 %copy-start.14 = (f32[1,8,64,128]{3,2,1,0:T(8,128)}, f32[1,8,64,128]{3,2,1,0:T(8,128)S(1)}, u32[]{:S(2)}) copy-start(f32[1,8,64,128]{3,2,1,0:T(8,128)S(1)} %copy.89) | copy-start | bytes 786436
  587.4 16.5 %copy-start.15 = (f32[1024,256]{1,0:T(8,128)S(1)}, f32[1024,256]{1,0:T(8,128)}, u32[]{:S(2)}) copy-start(f32[1024,256]{1,0:T(8,128)} %get-tuple-element.196) | copy-start | bytes 3145732
  597.6 13.2 %collective-permute-start.26 = (f32[64,1536]{1,0:T(8,128)}, f32[64,1536]{1,0:T(8,128)S(1)}, u32[]{:S(2)}, u32[]{:S(2)}) collective-permute-start(f32[64,1536]{1,0:T(8,128)} %get-tuple-element.176), channel_id=1, source_target_pairs={{0,4},{1,5},{2,6},{3,7},{4,0},{5,1},{6,2},{7,3},{8,12},{9,13},{10,... | collective-permute-start | bytes 1179656 | tf_op jit(solution)/shard_map/ppermute | solution.py:344
  599.3 12.2 %collective-permute-start.27 = (f32[64,1536]{1,0:T(8,128)}, f32[64,1536]{1,0:T(8,128)S(1)}, u32[]{:S(2)}, u32[]{:S(2)}) collective-permute-start(f32[64,1536]{1,0:T(8,128)} %get-tuple-element.177), channel_id=1, source_target_pairs={{0,2},{1,3},{2,0},{3,1},{4,6},{5,7},{6,4},{7,5},{8,10},{9,11},{10,... | collective-permute-start | bytes 1179656 | tf_op jit(solution)/shard_map/ppermute | solution.py:344
  600.7 14.8 %collective-permute-start.28 = (f32[64,1536]{1,0:T(8,128)}, f32[64,1536]{1,0:T(8,128)S(1)}, u32[]{:S(2)}, u32[]{:S(2)}) collective-permute-start(f32[64,1536]{1,0:T(8,128)} %get-tuple-element.178), channel_id=1, source_target_pairs={{0,4},{1,5},{2,6},{3,7},{4,0},{5,1},{6,2},{7,3},{8,12},{9,13},{10,... | collective-permute-start | bytes 1179656 | tf_op jit(solution)/shard_map/ppermute | solution.py:344
  601.2 15.7 %collective-permute-start.29 = (f32[64,1536]{1,0:T(8,128)}, f32[64,1536]{1,0:T(8,128)S(1)}, u32[]{:S(2)}, u32[]{:S(2)}) collective-permute-start(f32[64,1536]{1,0:T(8,128)} %get-tuple-element.179), channel_id=1, source_target_pairs={{0,2},{1,3},{2,0},{3,1},{4,6},{5,7},{6,4},{7,5},{8,10},{9,11},{10,... | collective-permute-start | bytes 1179656 | tf_op jit(solution)/shard_map/ppermute | solution.py:344
  603.9 5.4 collective-permute-start.30
  609.3 45.4 %collective-permute-start.39 = (f32[64,1024]{1,0:T(8,128)}, f32[64,1024]{1,0:T(8,128)}, u32[]{:S(2)}, u32[]{:S(2)}) collective-permute-start(f32[64,1024]{1,0:T(8,128)} %get-tuple-element.192), channel_id=1, source_target_pairs={{0,8},{8,0},{1,9},{9,1},{2,10},{10,2},{3,11},{11,3},{4,12},{12,4},... | collective-permute-start | bytes 786440 | tf_op jit(solution)/shard_map/ppermute | solution.py:396
  610.8 45.1 %collective-permute-start.38 = (f32[64,1024]{1,0:T(8,128)S(1)}, f32[64,1024]{1,0:T(8,128)}, u32[]{:S(2)}, u32[]{:S(2)}) collective-permute-start(f32[64,1024]{1,0:T(8,128)S(1)} %copy-done.26), channel_id=1, source_target_pairs={{0,8},{8,0},{1,9},{9,1},{2,10},{10,2},{3,11},{11,3},{4,12},{12,4},... | collective-permute-start | bytes 786440 | tf_op jit(solution)/shard_map/ppermute | solution.py:396
  623.1 4.5 collective-permute-start.35
  631.6 25.3 %collective-permute-start.36 = (f32[64,128]{1,0:T(8,128)}, f32[64,128]{1,0:T(8,128)S(1)}, u32[]{:S(2)}, u32[]{:S(2)}) collective-permute-start(f32[64,128]{1,0:T(8,128)} %moves.18), channel_id=1, source_target_pairs={{0,4},{1,5},{2,6},{3,7},{4,0},{5,1},{6,2},{7,3},{8,12},{9,13},{10,... | collective-permute-start | bytes 98312 | tf_op jit(solution)/shard_map/ppermute | solution.py:344
  660.9 6.5 collective-permute-start.37
  663.3 12.0 %collective-permute-start.34 = (f32[64,1536]{1,0:T(8,128)S(1)}, f32[64,1536]{1,0:T(8,128)S(1)}, u32[]{:S(2)}, u32[]{:S(2)}) collective-permute-start(f32[64,1536]{1,0:T(8,128)S(1)} %copy-done.23), channel_id=1, source_target_pairs={{0,8},{8,0},{1,9},{9,1},{2,10},{10,2},{3,11},{11,3},{4,12},{12,4},... | collective-permute-start | bytes 1179656 | tf_op jit(solution)/shard_map/ppermute | solution.py:396
  663.7 19.9 %collective-permute-start.33 = (f32[64,1536]{1,0:T(8,128)S(1)}, f32[64,1536]{1,0:T(8,128)S(1)}, u32[]{:S(2)}, u32[]{:S(2)}) collective-permute-start(f32[64,1536]{1,0:T(8,128)S(1)} %copy-done.22), channel_id=1, source_target_pairs={{0,8},{8,0},{1,9},{9,1},{2,10},{10,2},{3,11},{11,3},{4,12},{12,4},... | collective-permute-start | bytes 1179656 | tf_op jit(solution)/shard_map/ppermute | solution.py:396
  665.3 26.1 %collective-permute-start.32 = (f32[64,1536]{1,0:T(8,128)S(1)}, f32[64,1536]{1,0:T(8,128)S(1)}, u32[]{:S(2)}, u32[]{:S(2)}) collective-permute-start(f32[64,1536]{1,0:T(8,128)S(1)} %copy-done.21), channel_id=1, source_target_pairs={{0,8},{8,0},{1,9},{9,1},{2,10},{10,2},{3,11},{11,3},{4,12},{12,4},... | collective-permute-start | bytes 1179656 | tf_op jit(solution)/shard_map/ppermute | solution.py:396
  665.8 29.9 %collective-permute-start.31 = (f32[64,1536]{1,0:T(8,128)S(1)}, f32[64,1536]{1,0:T(8,128)S(1)}, u32[]{:S(2)}, u32[]{:S(2)}) collective-permute-start(f32[64,1536]{1,0:T(8,128)S(1)} %copy-done.20), channel_id=1, source_target_pairs={{0,8},{8,0},{1,9},{9,1},{2,10},{10,2},{3,11},{11,3},{4,12},{12,4},... | collective-permute-start | bytes 1179656 | tf_op jit(solution)/shard_map/ppermute | solution.py:396
  (31 other events, 141.4 us)
Sparse Core Ops, SparseCore 0:
  11.6 53.4 all-gather.6
  67.5 50.5 all-gather.8
  120.6 50.6 all-gather.10
where the time goes:
time: 711 us; the launch traced here: 705 us
  Pallas kernels  330 us (46%)
  waiting for transfers between devices  118 us (17%)
  local copies, waits for them, and re-layouts  97.8 us (14%)
  matrix products  56.4 us (8%)
  starting transfers between devices  40.2 us (6%)
  other arithmetic  35.8 us (5%)
  between operations  14.9 us (2%)
  blocking collectives  11.7 us (2%)
    pallas_call x2, Pallas kernels, mlp_chunk(): pl.pallas_call(mlp_kernel, grid=(cols // BLK,), in_specs=[whole((T, D)),...  145 us
    ppermute x33, waiting for transfers between devices, exchange(): return lax.ppermute(val, 'fsdp', [(i, i ^ bit) for i in range(NS)])  83.3 us
    pallas_call x2, Pallas kernels, attn_backward(): pl.pallas_call(attn_bwd_kernel, grid=(T // ROWS,), in_specs=[spec(3 * hal...  67.3 us
    pallas_call x10, Pallas kernels, advance(): pl.pallas_call(functools.partial(moves_kernel, [len(ins) for ins, _, _ in...  57.8 us
    unnamed x116, local copies, waits for them, and re-layouts  40.7 us
    ppermute x11, waiting for transfers between devices, start(): self.got4 = lax.ppermute(value, 'rep', [(0, 1), (1, 0)])  34.2 us
    dot_general x3, matrix products, dot_tn(): lax.dot_general(a, b, (((0,), (0,)), ((), ())), preferred_element_type=F32)  26.4 us
    ppermute x33, starting transfers between devices, exchange(): return lax.ppermute(val, 'fsdp', [(i, i ^ bit) for i in range(NS)])  26.3 us
  transfers between devices with their start and end apart: 47, of which 16 were waited for; matrix products, arithmetic and copies ran while one was open for 25% of the time, Pallas kernels for 46%

commit v1 on v0

--- a/solution.py
+++ b/solution.py
@@ -179,11 +179,11 @@
     )(qkv, qkv, qkv, d_heads)
 
 
-MLP_ROWS = 400
+MLP_ROWS = 800
 BLK = 2 * FC
 
 
-def mlp_kernel(h_ref, g_ref, ht_ref, gt_ref, w1_ref, wd_ref, b1_ref, m_ref, dh_ref,
+def mlp_kernel(h_ref, g_ref, ht_send, ht_keep, gt_ref, w1_ref, wd_ref, b1_ref, m_ref, dh_ref,
                gw1_send, gw1_keep, gw2_send, gw2_keep, gb_ref, act_s, dpre_s, w2_ref):
     step = pl.program_id(0)
     core = lax.rem(lax.axis_index("fsdp"), 2)
@@ -215,25 +215,28 @@
     lax.fori_loop(0, T // MLP_ROWS, rows_step, 0)
 
     def grad_step(i, carry):
-        for side, out in ((1 - core, gw1_send), (core, gw1_keep)):
-            rows = pl.ds(pl.multiple_of((2 * i + side) * 128, 128), 128)
-            out[i] = dot(ht_ref[rows, :], dpre_s[...])
-        rows = pl.ds(pl.multiple_of(i * 256, 256), 256)
+        for src, out in ((ht_send, gw1_send), (ht_keep, gw1_keep)):
+            two = pl.ds(2 * i, 2)
+            out[two] = dot(src[two].reshape(2 * D // NS, T), dpre_s[...]).reshape(2, D // NS, BLK)
+        rows = pl.ds(pl.multiple_of(i * (D // 2), D // 2), D // 2)
         for side, out in ((1 - core, gw2_send), (core, gw2_keep)):
             out[0, rows, :] = dot(gt_ref[rows, :], act_s[:, pl.ds(pl.multiple_of(side * FC, FC), FC)])
         return carry
 
-    lax.fori_loop(0, D // 256, grad_step, 0)
+    lax.fori_loop(0, 2, grad_step, 0)
 
 
 def mlp_chunk(h, g, ht, gt, weights, b1):
     cols = NS * FC
     once = pl.Buffered(1)
     whole = lambda shape: pl.BlockSpec(shape, lambda s: (0, 0), pipeline_mode=once)
+    core = lambda: lax.rem(lax.axis_index("fsdp"), 2)
+    half = lambda side: pl.BlockSpec((4, None, D // NS, T), lambda s: (0, side(), 0, 0), pipeline_mode=once)
+    ht = ht.reshape(4, 2, D // NS, T)
     return pl.pallas_call(
         mlp_kernel,
         grid=(cols // BLK,),
-        in_specs=[whole((T, D)), whole((T, D)), whole((D, T)), whole((D, T)),
+        in_specs=[whole((T, D)), whole((T, D)), half(lambda: 1 - core()), half(core), whole((D, T)),
                   pl.BlockSpec((NS, D // NS, BLK), lambda s: (0, 0, s)),
                   pl.BlockSpec((2, D // NS, cols), lambda s: (s, 1, 0)),
                   pl.BlockSpec((1, BLK), lambda s: (0, s))],
@@ -248,7 +251,7 @@
         compiler_params=pltpu.CompilerParams(dimension_semantics=("arbitrary",), vmem_limit_bytes=62 * 1024 * 1024),
         cost_estimate=pl.CostEstimate(flops=12 * T * D * cols, bytes_accessed=60_000_000, transcendentals=T * cols),
         name="mlp_fwd_bwd",
-    )(h, g, ht, gt, weights, weights, b1)
+    )(h, g, ht, ht, gt, weights, weights, b1)
 
 
 POST_ROWS = 200
@@ -514,31 +517,34 @@
             partial += [m_c, dh_c]
         partial = advance(partial, (mlp[0], "near"))
         z, g_resid, d_att_bf, vec_sums = post_mlp(partial[0], partial[2], partial[1], partial[3], x_flat, att, g_flat, vec)
+        z = row_major(z.reshape(SEQS, SEQ, D))
         d_heads = dot_nt(d_att_bf, wo).astype(BF16)
         out_red = split_full(dot_tn(heads, d_att_bf), 2)
 
         d_heads = advance(d_heads, (mlp[0], "far"), (mlp[1], "near"))
         d_qkv0, gb0 = attn_backward(qkv, d_heads, 0)
         qkv0 = split_full(dot_tn(h1, d_qkv0), 2)
-        d_qkv0, z = lax.optimization_barrier((d_qkv0, z))
-        z = row_major(z.reshape(SEQS, SEQ, D))
-        z, d_heads = advance((z, d_heads), (out_red, "near"), (mlp[0], "rep"))
-        d_heads = advance(d_heads, (mlp[1], "far"))
+        d_heads = advance(d_heads, (out_red, "near"), (mlp[0], "rep"))
+        d_heads = advance(d_heads, (mlp[1], "far"), (qkv0, "near"))
         d_qkv1, gb1 = attn_backward(qkv, d_heads, 1)
         gw1 = dot_tn(h1, d_qkv1)
         qkv1 = split_full(gw1, 2)
-        d_qkv1 = advance(d_qkv1, (qkv0, "near"), (out_red, "far"), (mlp[1], "rep"))
+        d_qkv1 = advance(d_qkv1, (qkv0, "far"), (out_red, "far"), (mlp[1], "rep"))
         d_qkv1 = advance(d_qkv1, (qkv1, "near"))
         dx, ln1_sums = ln1_backward(d_qkv0, d_qkv1, w_first, x_flat, g_resid, vec)
+        done = [(r.part, r.got4) for r in mlp[0]]
+        dx, z, done = lax.optimization_barrier((dx, z, done))
+        for r, (r.part, r.got4) in zip(mlp[0], done):
+            pass
         grad_vec = jnp.concatenate([ln1_sums[:2], vec_sums[2:]], axis=0)
         grad_bqkv = from_half(jnp.sum(jnp.concatenate([gb0, gb1], axis=2), axis=(0, 1))).reshape(NS, nq)
         grad_bup = jnp.stack(grad_bup, axis=1).reshape(NS, nu)
         grad_vec = grad_vec.reshape(8, NS, D // NS).transpose(1, 0, 2).reshape(NS, D)
         small_grads = jnp.concatenate([grad_bqkv, grad_bup, grad_vec, jnp.zeros((NS, 64 * 128 - nq - nu - D), F32)], axis=1)
         small_red = split_full(small_grads.reshape(NS * 64, 128), 1)
-        dx = advance(dx, (qkv1, "far"), (qkv0, "far"), (out_red, "rep"))
+        dx = advance(dx, (qkv1, "far"), (out_red, "rep"), (qkv0, "rep"))
         dx = row_major(dx.reshape(SEQS, SEQ, D))
-        advance((), (qkv1, "rep"), (qkv0, "rep"), (small_red, "near"))
+        advance((), (qkv1, "rep"), (small_red, "near"))
         advance((), (small_red, "far"))
         advance((), (small_red, "rep"))
         whole = lambda group: jnp.concatenate([r.result() for r in group], axis=0)

time: 711 us -> 681 us (0.958)
  waiting for transfers between devices: 118 us -> 93.1 us
    ppermute x11, waiting for transfers between devices: 34.2 us -> 12.3 us  [start(): self.got4 = lax.ppermute(value, 'rep', [(0, 1), (1, 0)])]
  transfers between devices with their start and end apart: 47 -> 47, of which waited for: 16 -> 9; matrix products, arithmetic and copies ran while one was open for 25% -> 26% of each run, Pallas kernels for 46% -> 48%
where the time goes in v1:
time: 681 us; the launch traced here: 675 us
  Pallas kernels  324 us (48%)
  local copies, waits for them, and re-layouts  101 us (15%)
  waiting for transfers between devices  93.1 us (14%)
  matrix products  55.4 us (8%)
  starting transfers between devices  39.2 us (6%)
  other arithmetic  36.1 us (5%)
  between operations  14.8 us (2%)
  blocking collectives  11.3 us (2%)
    pallas_call x2, Pallas kernels, mlp_chunk(): pl.pallas_call(mlp_kernel, grid=(cols // BLK,), in_specs=[whole((T, D)),...  138 us
    ppermute x33, waiting for transfers between devices, exchange(): return lax.ppermute(val, 'fsdp', [(i, i ^ bit) for i in range(NS)])  80.7 us
    pallas_call x2, Pallas kernels, attn_backward(): pl.pallas_call(attn_bwd_kernel, grid=(T // ROWS,), in_specs=[spec(3 * hal...  67.1 us
    pallas_call x10, Pallas kernels, advance(): pl.pallas_call(functools.partial(moves_kernel, [len(ins) for ins, _, _ in...  57.7 us
    unnamed x116, local copies, waits for them, and re-layouts  44.5 us
    ppermute x33, starting transfers between devices, exchange(): return lax.ppermute(val, 'fsdp', [(i, i ^ bit) for i in range(NS)])  26.2 us
    dot_general x3, matrix products, dot_tn(): lax.dot_general(a, b, (((0,), (0,)), ((), ())), preferred_element_type=F32)  25.5 us
    dot_general x2, matrix products, dot(): lax.dot_general(a, b, (((1,), (0,)), ((), ())), preferred_element_type=F32)  23.4 us
  transfers between devices with their start and end apart: 47, of which 9 were waited for; matrix products, arithmetic and copies ran while one was open for 26% of the time, Pallas kernels for 48%

profile of v1, /device:TPU:0, one launch (start us, length us, event | category | flops | bytes accessed | tf_op | source)
XLA Modules:
  0.0 674.5 jit_solution(246239573874536217)
XLA Ops:
  8.3 1.8 copy.63
  11.6 1.9 convert.36
  14.7 5.1 slice_reduce_fusion
  23.1 2.0 maximum_maximum_fusion.2
  25.3 11.3 %all-gather.2 = bf16[8,1,1920]{2,1,0:T(2,128)(2,1)S(1)} all-gather(bf16[1,1,1920]{2,1,0:T(2,128)(2,1)S(1)} %maximum_bitcast_fusion.2), channel_id=1, replica_groups=mesh['rep'=2,'fsdp'=8] {'fsdp'}, dimensions={0}, use_global_device_ids=true | all-gather | bytes 34560 | tf_op jit(solution)/shard_map/all_gather | solution.py:483
  36.7 3.7 copy.61
  40.4 3.2 reshape.203.x_ref
  43.6 6.8 %copy.67 = bf16[32,50,1024]{2,1,0:T(8,128)(2,1)} copy(bf16[32,50,1024]{2,0,1:T(8,128)(2,1)} %param.10) | data formatting | bytes 6553600 | tf_op args[1]
  50.3 4.8 reshape.207.g_ref
  55.2 4.6 multiply_convert_fusion.g_ref
  59.8 5.5 copy.69
  68.1 16.4 %add_convert_fusion.q_ref.k_ref.v_ref = bf16[1600,3072]{1,0:T(8,128)(2,1)} fusion(f32[3072]{0:T(1024)S(1)} %add.111, bf16[1024,4096]{1,0:T(8,128)(2,1)} %all-gather.7.cloned.1.call-done.w_ref, bf16[1600,1024]{1,0:T(8,128)(2,1)S(1)} %reshape.203.x_ref, f32[1024]{0:T(1024)S(1)} %bitcast.217, f32[1024]{0:T(1024)S(1)} %bitcast.220, f32[1600]{0:T(1024)S(1)} %add_rsqrt_fusion.1, ...), kind=kOutput, calls=%fused_computation | convolution fusion | flops 10085990400 | bytes 19431936 | tf_op jit(solution)/shard_map/dot_general | solution.py:38
  84.5 20.8 %attn_fwd.1 = bf16[1600,1024]{1,0:T(8,128)(2,1)} custom-call(bf16[1600,3072]{1,0:T(8,128)(2,1)} %add_convert_fusion.q_ref.k_ref.v_ref, bf16[1600,3072]{1,0:T(8,128)(2,1)} %add_convert_fusion.q_ref.k_ref.v_ref, bf16[1600,3072]{1,0:T(8,128)(2,1)} %add_convert_fusion.q_ref.k_ref.v_ref), custom_call_target="tpu_custom_call" | custom-call | flops 8000000000 | bytes 13000000 | tf_op jit(solution)/shard_map/attn_fwd/pallas_call | solution.py:156
  105.3 7.0 %fusion.9 = (f32[1600]{0:T(1024)S(1)}, f32[1600,1024]{1,0:T(8,128)S(1)}) fusion(f32[1024]{0:T(1024)S(1)} %bitcast.204, bf16[1600,1024]{1,0:T(8,128)(2,1)S(1)} %reshape.203.x_ref, f32[1024]{0:T(1024)S(1)} %bitcast.223, bf16[1600,1024]{1,0:T(8,128)(2,1)} %attn_fwd.1, bf16[1024,4096]{1,0:T(8,128)(2,1)} %all-gather.7.cloned.1.call-done.w_ref), kind=kOutput, calls=%fused_computation.20 | convolution fusion | flops 3363633664 | bytes 15218944 | tf_op jit(solution)/shard_map/dot_general | solution.py:38
  115.0 3.1 add_convert_fusion.1.h_ref
  118.2 5.4 copy.68
  123.6 69.5 %mlp_fwd_bwd.2 = (f32[1600,1024]{1,0:T(8,128)}, f32[1600,1024]{1,0:T(8,128)}, f32[4,128,2048]{2,1,0:T(8,128)}, f32[4,128,2048]{2,1,0:T(8,128)}, f32[4,1024,256]{...) custom-call(bf16[1600,1024]{1,0:T(8,128)(2,1)} %add_convert_fusion.1.h_ref, ...), custom_call_target="tpu_custom_call" | custom-call | flops 40265318400 | bytes 60000000 | tf_op jit(solution)/shard_map/mlp_fwd_bwd/pallas_call | solution.py:236
  193.7 68.9 %mlp_fwd_bwd.3 = (f32[1600,1024]{1,0:T(8,128)}, f32[1600,1024]{1,0:T(8,128)}, f32[4,128,2048]{2,1,0:T(8,128)}, f32[4,128,2048]{2,1,0:T(8,128)}, f32[4,1024,256]{...) custom-call(bf16[1600,1024]{1,0:T(8,128)(2,1)} %add_convert_fusion.1.h_ref, ...), custom_call_target="tpu_custom_call" | custom-call | flops 40265318400 | bytes 60000000 | tf_op jit(solution)/shard_map/mlp_fwd_bwd/pallas_call | solution.py:236
  263.8 6.4 moves.10
  270.2 1.8 collective-permute-start.2
  272.7 20.1 %post_mlp.1 = (bf16[1600,1024]{1,0:T(8,128)(2,1)}, f32[1600,1024]{1,0:T(8,128)}, bf16[1600,1024]{1,0:T(8,128)(2,1)}, f32[8,1024]{1,0:T(8,128)}) custom-call(f32[1600,1024]{1,0:T(8,128)} %get-tuple-element.118.m0_ref, f32[1600,1024]{1,0:T(8,128)} %get-tuple-element.119.m1_ref, f32[1600,1024]{1,0:T(8,128)} %get-tuple-element.120.d0_ref, ...), custom_call_target="tpu_custom_call" | custom-call | flops 5000000000 | bytes 56000000 | tf_op jit(solution)/shard_map/post_mlp/pallas_call | solution.py:285
  292.8 6.9 %fusion.19 = f32[1024,1024]{1,0:T(8,128)S(1)} fusion(bf16[1600,1024]{1,0:T(8,128)(2,1)} %attn_fwd.1, bf16[1600,1024]{1,0:T(8,128)(2,1)} %get-tuple-element.122), kind=kOutput, calls=%fused_computation.70 | convolution fusion | flops 3355443200 | bytes 10747904 | tf_op jit(solution)/shard_map/dot_general | solution.py:46
  304.4 6.5 convolution_convert_fusion.g_ref
  311.0 7.1 %collective-permute-done.2.refs_2_.refs_6_ = f32[2,128,2048]{2,1,0:T(8,128)S(1)} collective-permute-done((f32[2,128,2048]{2,1,0:T(8,128)}, f32[2,128,2048]{2,1,0:T(8,128)S(1)}, u32[]{:S(2)}, u32[]{:S(2)}) %collective-permute-start.2) | collective-permute-done | bytes 2097184 | tf_op jit(solution)/shard_map/ppermute | solution.py:347
  319.6 8.6 %moves.11 = (f32[128,2048]{1,0:T(8,128)}, f32[1024,256]{1,0:T(8,128)}, f32[2,128,2048]{2,1,0:T(8,128)}, f32[2,1024,256]{2,1,0:T(8,128)}) custom-call(s32[3]{0:T(128)} %pad_add_fusion.idx_ref, f32[2,2,1,128,2048]{4,3,2,1,0:T(8,128)} %bitcast.158, f32[2,2,128,2048]{3,2,1,0:T(8,128)} %collective-permute-done.refs_1_.refs_5_, f32[2,128,2048]{2,1,0:T(8,128)} %copy-done.8, ...), custom_call_target="tpu_custom_call" | custom-call | flops 1000000000 | bytes 10000000 | tf_op jit(solution)/shard_map/moves/pallas_call | solution.py:424
  328.3 33.6 %attn_bwd.2 = (bf16[1600,1536]{1,0:T(8,128)(2,1)}, f32[4,1,1536]{2,1,0:T(1,128)}) custom-call(bf16[1600,3072]{1,0:T(8,128)(2,1)} %add_convert_fusion.q_ref.k_ref.v_ref, bf16[1600,3072]{1,0:T(8,128)(2,1)} %add_convert_fusion.q_ref.k_ref.v_ref, bf16[1600,3072]{1,0:T(8,128)(2,1)} %add_convert_fusion.q_ref.k_ref.v_ref, ...), custom_call_target="tpu_custom_call" | custom-call | flops 16000000000 | bytes 12000000 | tf_op jit(solution)/shard_map/attn_bwd/pallas_call | solution.py:170
  361.9 1.6 collective-permute-start.8
  365.4 9.2 %fusion.12 = f32[1024,1536]{1,0:T(8,128)S(1)} fusion(bf16[1600,1536]{1,0:T(8,128)(2,1)} %get-tuple-element.134.d0_ref, bf16[1600,1024]{1,0:T(8,128)(2,1)S(1)} %copy-done.4, f32[1024]{0:T(1024)S(1)} %bitcast.218, f32[1024]{0:T(1024)S(1)} %bitcast.221, f32[1600]{0:T(1024)S(1)} %copy-done.37, f32[1600]{0:T(1024)S(1)} %copy-done.29), kind=kOutput, calls=%fused_computation.63 | convolution fusion | flops 5042995200 | bytes 14504448 | tf_op jit(solution)/shard_map/dot_general | solution.py:46
  375.2 2.1 copy-done
  380.4 7.9 %collective-permute-done.8.refs_7_ = f32[128,2048]{1,0:T(8,128)} collective-permute-done((f32[128,2048]{1,0:T(8,128)}, f32[128,2048]{1,0:T(8,128)}, u32[]{:S(2)}, u32[]{:S(2)}) %collective-permute-start.8) | collective-permute-done | bytes 1048608 | tf_op jit(solution)/shard_map/ppermute | solution.py:347
  389.7 43.3 %collective-permute-done.9.refs_11_ = f32[1024,256]{1,0:T(8,128)} collective-permute-done((f32[1024,256]{1,0:T(8,128)S(1)}, f32[1024,256]{1,0:T(8,128)}, u32[]{:S(2)}, u32[]{:S(2)}) %collective-permute-start.9) | collective-permute-done | bytes 1048608 | tf_op jit(solution)/shard_map/ppermute | solution.py:347
  433.0 6.7 moves.12
  441.5 6.5 moves.13
  448.1 33.5 %attn_bwd.3 = (bf16[1600,1536]{1,0:T(8,128)(2,1)}, f32[4,1,1536]{2,1,0:T(1,128)}) custom-call(bf16[1600,3072]{1,0:T(8,128)(2,1)} %add_convert_fusion.q_ref.k_ref.v_ref, bf16[1600,3072]{1,0:T(8,128)(2,1)} %add_convert_fusion.q_ref.k_ref.v_ref, bf16[1600,3072]{1,0:T(8,128)(2,1)} %add_convert_fusion.q_ref.k_ref.v_ref, ...), custom_call_target="tpu_custom_call" | custom-call | flops 16000000000 | bytes 12000000 | tf_op jit(solution)/shard_map/attn_bwd/pallas_call | solution.py:170
  482.2 1.7 collective-permute-start.15
  484.3 9.3 %fusion.10 = f32[1024,1536]{1,0:T(8,128)S(1)} fusion(bf16[1600,1536]{1,0:T(8,128)(2,1)} %get-tuple-element.165.d1_ref, bf16[1600,1024]{1,0:T(8,128)(2,1)S(1)} %copy-done.4, f32[1024]{0:T(1024)S(1)} %bitcast.219, f32[1024]{0:T(1024)S(1)} %bitcast.222, f32[1600]{0:T(1024)S(1)} %copy-done.37, f32[1600]{0:T(1024)S(1)} %copy-done.29), kind=kOutput, calls=%fused_computation.62 | convolution fusion | flops 5042995200 | bytes 14504448 | tf_op jit(solution)/shard_map/dot_general | solution.py:46
  494.2 2.0 copy-done.1
  500.7 2.3 collective-permute-done.15.refs_5_.refs_20_
  504.5 17.5 %collective-permute-done.18.refs_15_ = f32[128,2048]{1,0:T(8,128)} collective-permute-done((f32[128,2048]{1,0:T(8,128)}, f32[128,2048]{1,0:T(8,128)}, u32[]{:S(2)}, u32[]{:S(2)}) %collective-permute-start.18) | collective-permute-done | bytes 1048608 | tf_op jit(solution)/shard_map/ppermute | solution.py:347
  524.5 7.4 %moves.14 = (f32[64,1536]{1,0:T(8,128)}, f32[64,1536]{1,0:T(8,128)}, f32[64,1024]{1,0:T(8,128)}, f32[64,1024]{1,0:T(8,128)}, f32[128,2048]{1,0:T(8,128)}, /*index=5*/f32[1024,256]{1,0:T(8,128)}) custom-call(s32[3]{0:T(128)} %pad_add_fusion.idx_ref, f32[2,2,2,128,1536]{4,3,2,1,0:T(8,128)} %bitcast.139, ...), custom_call_target="tpu_custom_call" | custom-call | flops 1000000000 | bytes 10000000 | tf_op jit(solution)/shard_map/moves/pallas_call | solution.py:424
  531.9 1.7 collective-permute-start.26
  534.4 4.7 reshape.224
  542.8 4.7 moves.15
  550.9 19.7 %ln1_back.1 = (bf16[1600,1024]{1,0:T(8,128)(2,1)}, f32[8,1024]{1,0:T(8,128)}) custom-call(bf16[1600,1536]{1,0:T(8,128)(2,1)} %get-tuple-element.134.d0_ref, bf16[1600,1536]{1,0:T(8,128)(2,1)} %get-tuple-element.165.d1_ref, bf16[1024,4096]{1,0:T(8,128)(2,1)} %all-gather.7.cloned.1.call-done.w_ref, bf16[1600,1024]{1,0:T(8,128)(2,1)} %copy-done.3, ...), custom_call_target="tpu_custom_call" | custom-call | flops 10066329600 | bytes 30000000 | tf_op jit(solution)/shard_map/ln1_back/pallas_call | solution.py:329
  574.3 5.5 copy.76
  579.9 1.8 add_bitcast_fusion.1
  584.3 6.0 moves.16
  591.5 1.7 add.130
  594.5 2.4 add_bitcast_fusion
  596.9 1.7 add.131
  603.4 4.6 moves.17
  609.2 1.7 pad_maximum_fusion
  613.0 3.3 moves.18
  616.3 1.9 collective-permute-start.38
  618.2 2.8 pad_maximum_fusion.1
  621.0 3.0 copy.75
  624.0 4.0 reshape.232
  628.0 1.8 copy.79
  629.8 4.6 reshape.225
  634.4 5.5 copy.77
  642.2 3.4 moves.19
  653.2 5.9 collective-permute-done.36
  659.2 6.3 collective-permute-done.35
  666.2 1.6 copy.78
  (257 shorter events, 75.4 us)
Async XLA Ops:
  7.2 60.9 %all-gather.7.cloned.1.call-start = ((), (), s32[]{:S(2)}) async-start(), calls=%async_computation | async-start | bytes 9437184 | tf_op jit(solution)/shard_map/all_gather | solution.py:343
  11.5 112.1 %all-gather.9.cloned.1.call-start = ((), (), s32[]{:S(2)}) async-start(), calls=%async_computation.1 | async-start | bytes 9437184 | tf_op jit(solution)/shard_map/all_gather | solution.py:481
  21.7 14.9 %copy-start.10 = (bf16[32,50,1024]{2,0,1:T(8,128)(2,1)S(1)}, bf16[32,50,1024]{2,0,1:T(8,128)(2,1)}, u32[]{:S(2)}) copy-start(bf16[32,50,1024]{2,0,1:T(8,128)(2,1)} %param.9) | copy-start | bytes 9830404
  21.8 171.9 %all-gather.11.cloned.1.call-start = ((), (), s32[]{:S(2)}) async-start(), calls=%async_computation.2 | async-start | bytes 9437184 | tf_op jit(solution)/shard_map/all_gather | solution.py:481
  43.5 70.3 %copy-start.3 = (bf16[1600,1024]{1,0:T(8,128)(2,1)}, bf16[1600,1024]{1,0:T(8,128)(2,1)S(1)}, u32[]{:S(2)}) copy-start(bf16[1600,1024]{1,0:T(8,128)(2,1)S(1)} %reshape.203.x_ref) | copy-start | bytes 9830404
  43.6 11.5 %copy-start.23 = (f32[8,8,128]{2,1,0:T(8,128)}, f32[8,8,128]{2,1,0:T(8,128)S(1)}, u32[]{:S(2)}) copy-start(f32[8,8,128]{2,1,0:T(8,128)S(1)} %copy.103) | copy-start | bytes 98308
  55.1 12.9 %copy-start.38 = (f32[1,8,128]{2,0,1:T(1,128)}, f32[1,8,128]{2,0,1:T(1,128)S(1)}, u32[]{:S(2)}) copy-start(f32[1,8,128]{2,0,1:T(1,128)S(1)} %get-tuple-element.262) | copy-start | bytes 12292
  55.1 12.9 %copy-start.40 = (f32[1,8,128]{2,0,1:T(1,128)}, f32[1,8,128]{2,0,1:T(1,128)S(1)}, u32[]{:S(2)}) copy-start(f32[1,8,128]{2,0,1:T(1,128)S(1)} %get-tuple-element.263) | copy-start | bytes 12292
  67.0 17.5 %copy-start.28 = (f32[1600]{0:T(1024)}, f32[1600]{0:T(1024)S(1)}, u32[]{:S(2)}) copy-start(f32[1600]{0:T(1024)S(1)} %broadcast_multiply_fusion.1) | copy-start | bytes 19204
  68.0 16.5 %copy-start.36 = (f32[1600]{0:T(1024)}, f32[1600]{0:T(1024)S(1)}, u32[]{:S(2)}) copy-start(f32[1600]{0:T(1024)S(1)} %add_rsqrt_fusion.1) | copy-start | bytes 19204
  193.1 70.7 %collective-permute-start = (f32[2,2,128,2048]{3,2,1,0:T(8,128)}, f32[2,2,128,2048]{3,2,1,0:T(8,128)}, u32[]{:S(2)}, u32[]{:S(2)}) collective-permute-start(f32[2,2,128,2048]{3,2,1,0:T(8,128)} %bitcast.231), channel_id=1, source_target_pairs={{0,1},{1,0},{2,3},{3,2},{4,5},{5,4},{6,7},{7,6},{8,9},{9,8},{10,11... | collective-permute-start | bytes 12582920 | tf_op jit(solution)/shard_map/ppermute | solution.py:347
  193.2 70.5 %collective-permute-start.1 = (f32[2,2,1024,256]{3,2,1,0:T(8,128)}, f32[2,2,1024,256]{3,2,1,0:T(8,128)}, u32[]{:S(2)}, u32[]{:S(2)}) collective-permute-start(f32[2,2,1024,256]{3,2,1,0:T(8,128)} %bitcast.230), channel_id=1, source_target_pairs={{0,1},{1,0},{2,3},{3,2},{4,5},{5,4},{6,7},{7,6},{8,9},{9,8},{10,11... | collective-permute-start | bytes 12582920 | tf_op jit(solution)/shard_map/ppermute | solution.py:347
  262.5 48.4 %collective-permute-start.4 = (f32[2,2,128,2048]{3,2,1,0:T(8,128)}, f32[2,2,128,2048]{3,2,1,0:T(8,128)}, u32[]{:S(2)}, u32[]{:S(2)}) collective-permute-start(f32[2,2,128,2048]{3,2,1,0:T(8,128)} %bitcast.229), channel_id=1, source_target_pairs={{0,1},{1,0},{2,3},{3,2},{4,5},{5,4},{6,7},{7,6},{8,9},{9,8},{10,11... | collective-permute-start | bytes 12582920 | tf_op jit(solution)/shard_map/ppermute | solution.py:347
  262.7 48.3 %collective-permute-start.5 = (f32[2,2,1024,256]{3,2,1,0:T(8,128)}, f32[2,2,1024,256]{3,2,1,0:T(8,128)}, u32[]{:S(2)}, u32[]{:S(2)}) collective-permute-start(f32[2,2,1024,256]{3,2,1,0:T(8,128)} %bitcast.228), channel_id=1, source_target_pairs={{0,1},{1,0},{2,3},{3,2},{4,5},{5,4},{6,7},{7,6},{8,9},{9,8},{10,11... | collective-permute-start | bytes 12582920 | tf_op jit(solution)/shard_map/ppermute | solution.py:347
  270.2 47.9 %collective-permute-start.2 = (f32[2,128,2048]{2,1,0:T(8,128)}, f32[2,128,2048]{2,1,0:T(8,128)S(1)}, u32[]{:S(2)}, u32[]{:S(2)}) collective-permute-start(f32[2,128,2048]{2,1,0:T(8,128)} %get-tuple-element.123), channel_id=1, source_target_pairs={{0,2},{1,3},{2,0},{3,1},{4,6},{5,7},{6,4},{7,5},{8,10},{9,11},{10,... | collective-permute-start | bytes 6291464 | tf_op jit(solution)/shard_map/ppermute | solution.py:347
  272.0 47.6 %collective-permute-start.3 = (f32[2,1024,256]{2,1,0:T(8,128)}, f32[2,1024,256]{2,1,0:T(8,128)}, u32[]{:S(2)}, u32[]{:S(2)}) collective-permute-start(f32[2,1024,256]{2,1,0:T(8,128)} %get-tuple-element.124), channel_id=1, source_target_pairs={{0,4},{1,5},{2,6},{3,7},{4,0},{5,1},{6,2},{7,3},{8,12},{9,13},{10,... | collective-permute-start | bytes 6291464 | tf_op jit(solution)/shard_map/ppermute | solution.py:347
  302.8 75.7 %collective-permute-start.6 = (f32[2,2,64,1024]{3,2,1,0:T(8,128)}, f32[2,2,64,1024]{3,2,1,0:T(8,128)}, u32[]{:S(2)}, u32[]{:S(2)}) collective-permute-start(f32[2,2,64,1024]{3,2,1,0:T(8,128)} %dynamic-slice_bitcast_fusion.5), channel_id=1, source_target_pairs={{0,1},{1,0},{2,3},{3,2},{4,5},{5,4},{6,7},{7,6},{8,9},{9,8},{10,11... | collective-permute-start | bytes 3145736 | tf_op jit(solution)/shard_map/ppermute | solution.py:347
  310.9 68.9 %collective-permute-start.7 = (f32[2,2,64,1024]{3,2,1,0:T(8,128)}, f32[2,2,64,1024]{3,2,1,0:T(8,128)}, u32[]{:S(2)}, u32[]{:S(2)}) collective-permute-start(f32[2,2,64,1024]{3,2,1,0:T(8,128)} %dynamic-slice_bitcast_fusion.4), channel_id=1, source_target_pairs={{0,1},{1,0},{2,3},{3,2},{4,5},{5,4},{6,7},{7,6},{8,9},{9,8},{10,11... | collective-permute-start | bytes 3145736 | tf_op jit(solution)/shard_map/ppermute | solution.py:347
  328.2 37.2 %copy-start.4 = (bf16[1600,1024]{1,0:T(8,128)(2,1)S(1)}, bf16[1600,1024]{1,0:T(8,128)(2,1)}, u32[]{:S(2)}) copy-start(bf16[1600,1024]{1,0:T(8,128)(2,1)} %copy-done.3) | copy-start | bytes 9830404
  328.2 37.2 %copy-start.29 = (f32[1600]{0:T(1024)S(1)}, f32[1600]{0:T(1024)}, u32[]{:S(2)}) copy-start(f32[1600]{0:T(1024)} %copy-done.28) | copy-start | bytes 19204
  328.2 37.2 %copy-start.37 = (f32[1600]{0:T(1024)S(1)}, f32[1600]{0:T(1024)}, u32[]{:S(2)}) copy-start(f32[1600]{0:T(1024)} %copy-done.36) | copy-start | bytes 19204
  328.2 37.2 %copy-start.39 = (f32[1,8,128]{2,0,1:T(1,128)S(1)}, f32[1,8,128]{2,0,1:T(1,128)}, u32[]{:S(2)}) copy-start(f32[1,8,128]{2,0,1:T(1,128)} %copy-done.38) | copy-start | bytes 12292
  328.2 37.2 %copy-start.41 = (f32[1,8,128]{2,0,1:T(1,128)S(1)}, f32[1,8,128]{2,0,1:T(1,128)}, u32[]{:S(2)}) copy-start(f32[1,8,128]{2,0,1:T(1,128)} %copy-done.40) | copy-start | bytes 12292
  361.9 26.3 %collective-permute-start.8 = (f32[128,2048]{1,0:T(8,128)}, f32[128,2048]{1,0:T(8,128)}, u32[]{:S(2)}, u32[]{:S(2)}) collective-permute-start(f32[128,2048]{1,0:T(8,128)} %get-tuple-element.135), channel_id=1, source_target_pairs={{0,4},{1,5},{2,6},{3,7},{4,0},{5,1},{6,2},{7,3},{8,12},{9,13},{10,... | collective-permute-start | bytes 3145736 | tf_op jit(solution)/shard_map/ppermute | solution.py:347
  363.5 78.0 %collective-permute-start.10 = (f32[2,128,2048]{2,1,0:T(8,128)}, f32[2,128,2048]{2,1,0:T(8,128)}, u32[]{:S(2)}, u32[]{:S(2)}) collective-permute-start(f32[2,128,2048]{2,1,0:T(8,128)} %get-tuple-element.142), channel_id=1, source_target_pairs={{0,2},{1,3},{2,0},{3,1},{4,6},{5,7},{6,4},{7,5},{8,10},{9,11},{10,... | collective-permute-start | bytes 6291464 | tf_op jit(solution)/shard_map/ppermute | solution.py:347
  364.5 77.0 %collective-permute-start.11 = (f32[2,1024,256]{2,1,0:T(8,128)}, f32[2,1024,256]{2,1,0:T(8,128)}, u32[]{:S(2)}, u32[]{:S(2)}) collective-permute-start(f32[2,1024,256]{2,1,0:T(8,128)} %get-tuple-element.143), channel_id=1, source_target_pairs={{0,4},{1,5},{2,6},{3,7},{4,0},{5,1},{6,2},{7,3},{8,12},{9,13},{10,... | collective-permute-start | bytes 6291464 | tf_op jit(solution)/shard_map/ppermute | solution.py:347
  378.6 62.5 %collective-permute-start.12 = (f32[2,2,64,1536]{3,2,1,0:T(8,128)}, f32[2,2,64,1536]{3,2,1,0:T(8,128)}, u32[]{:S(2)}, u32[]{:S(2)}) collective-permute-start(f32[2,2,64,1536]{3,2,1,0:T(8,128)} %dynamic-slice_bitcast_fusion.3), channel_id=1, source_target_pairs={{0,1},{1,0},{2,3},{3,2},{4,5},{5,4},{6,7},{7,6},{8,9},{9,8},{10,11... | collective-permute-start | bytes 4718600 | tf_op jit(solution)/shard_map/ppermute | solution.py:347
  379.8 61.7 %collective-permute-start.13 = (f32[2,2,64,1536]{3,2,1,0:T(8,128)}, f32[2,2,64,1536]{3,2,1,0:T(8,128)}, u32[]{:S(2)}, u32[]{:S(2)}) collective-permute-start(f32[2,2,64,1536]{3,2,1,0:T(8,128)} %dynamic-slice_bitcast_fusion.2), channel_id=1, source_target_pairs={{0,1},{1,0},{2,3},{3,2},{4,5},{5,4},{6,7},{7,6},{8,9},{9,8},{10,11... | collective-permute-start | bytes 4718600 | tf_op jit(solution)/shard_map/ppermute | solution.py:347
  388.2 44.8 %collective-permute-start.9 = (f32[1024,256]{1,0:T(8,128)S(1)}, f32[1024,256]{1,0:T(8,128)}, u32[]{:S(2)}, u32[]{:S(2)}) collective-permute-start(f32[1024,256]{1,0:T(8,128)S(1)} %copy-done.47), channel_id=1, source_target_pairs={{0,2},{1,3},{2,0},{3,1},{4,6},{5,7},{6,4},{7,5},{8,10},{9,11},{10,... | collective-permute-start | bytes 3145736 | tf_op jit(solution)/shard_map/ppermute | solution.py:347
  439.8 57.8 %collective-permute-start.16 = (f32[2,64,1024]{2,1,0:T(8,128)}, f32[2,64,1024]{2,1,0:T(8,128)}, u32[]{:S(2)}, u32[]{:S(2)}) collective-permute-start(f32[2,64,1024]{2,1,0:T(8,128)} %get-tuple-element.152), channel_id=1, source_target_pairs={{0,2},{1,3},{2,0},{3,1},{4,6},{5,7},{6,4},{7,5},{8,10},{9,11},{10,... | collective-permute-start | bytes 1572872 | tf_op jit(solution)/shard_map/ppermute | solution.py:347
  441.1 57.7 %collective-permute-start.17 = (f32[2,64,1024]{2,1,0:T(8,128)}, f32[2,64,1024]{2,1,0:T(8,128)}, u32[]{:S(2)}, u32[]{:S(2)}) collective-permute-start(f32[2,64,1024]{2,1,0:T(8,128)} %get-tuple-element.153), channel_id=1, source_target_pairs={{0,4},{1,5},{2,6},{3,7},{4,0},{5,1},{6,2},{7,3},{8,12},{9,13},{10,... | collective-permute-start | bytes 1572872 | tf_op jit(solution)/shard_map/ppermute | solution.py:347
  481.6 17.7 %collective-permute-start.14 = (f32[2,64,1536]{2,1,0:T(8,128)}, f32[2,64,1536]{2,1,0:T(8,128)}, u32[]{:S(2)}, u32[]{:S(2)}) collective-permute-start(f32[2,64,1536]{2,1,0:T(8,128)} %get-tuple-element.150), channel_id=1, source_target_pairs={{0,2},{1,3},{2,0},{3,1},{4,6},{5,7},{6,4},{7,5},{8,10},{9,11},{10,... | collective-permute-start | bytes 2359304 | tf_op jit(solution)/shard_map/ppermute | solution.py:347
  482.2 20.7 %collective-permute-start.15 = (f32[2,64,1536]{2,1,0:T(8,128)}, f32[2,64,1536]{2,1,0:T(8,128)}, u32[]{:S(2)}, u32[]{:S(2)}) collective-permute-start(f32[2,64,1536]{2,1,0:T(8,128)} %get-tuple-element.151), channel_id=1, source_target_pairs={{0,4},{1,5},{2,6},{3,7},{4,0},{5,1},{6,2},{7,3},{8,12},{9,13},{10,... | collective-permute-start | bytes 2359304 | tf_op jit(solution)/shard_map/ppermute | solution.py:347
  483.9 38.0 %collective-permute-start.18 = (f32[128,2048]{1,0:T(8,128)}, f32[128,2048]{1,0:T(8,128)}, u32[]{:S(2)}, u32[]{:S(2)}) collective-permute-start(f32[128,2048]{1,0:T(8,128)} %get-tuple-element.154), channel_id=1, source_target_pairs={{0,4},{1,5},{2,6},{3,7},{4,0},{5,1},{6,2},{7,3},{8,12},{9,13},{10,... | collective-permute-start | bytes 3145736 | tf_op jit(solution)/shard_map/ppermute | solution.py:347
  497.5 42.9 %collective-permute-start.20 = (f32[2,2,64,1536]{3,2,1,0:T(8,128)}, f32[2,2,64,1536]{3,2,1,0:T(8,128)S(1)}, u32[]{:S(2)}, u32[]{:S(2)}) collective-permute-start(f32[2,2,64,1536]{3,2,1,0:T(8,128)} %dynamic-slice_bitcast_fusion.1), channel_id=1, source_target_pairs={{0,1},{1,0},{2,3},{3,2},{4,5},{5,4},{6,7},{7,6},{8,9},{9,8},{10,11... | collective-permute-start | bytes 4718600 | tf_op jit(solution)/shard_map/ppermute | solution.py:347
  498.8 35.5 %copy-start.35 = (f32[1,2048]{1,0:T(1,128)S(1)}, f32[1,2048]{1,0:T(1,128)}, u32[]{:S(2)}) copy-start(f32[1,2048]{1,0:T(1,128)} %get-tuple-element.193) | copy-start | bytes 24580
  498.8 35.5 %copy-start.34 = (f32[1,2048]{1,0:T(1,128)S(1)}, f32[1,2048]{1,0:T(1,128)}, u32[]{:S(2)}) copy-start(f32[1,2048]{1,0:T(1,128)} %get-tuple-element.192) | copy-start | bytes 24580
  498.8 42.9 %collective-permute-start.21 = (f32[2,2,64,1536]{3,2,1,0:T(8,128)}, f32[2,2,64,1536]{3,2,1,0:T(8,128)S(1)}, u32[]{:S(2)}, u32[]{:S(2)}) collective-permute-start(f32[2,2,64,1536]{3,2,1,0:T(8,128)} %dynamic-slice_bitcast_fusion), channel_id=1, source_target_pairs={{0,1},{1,0},{2,3},{3,2},{4,5},{5,4},{6,7},{7,6},{8,9},{9,8},{10,11... | collective-permute-start | bytes 4718600 | tf_op jit(solution)/shard_map/ppermute | solution.py:347
  499.3 25.2 %collective-permute-start.19 = (f32[1024,256]{1,0:T(8,128)S(1)}, f32[1024,256]{1,0:T(8,128)}, u32[]{:S(2)}, u32[]{:S(2)}) collective-permute-start(f32[1024,256]{1,0:T(8,128)S(1)} %copy-done.46), channel_id=1, source_target_pairs={{0,2},{1,3},{2,0},{3,1},{4,6},{5,7},{6,4},{7,5},{8,10},{9,11},{10,... | collective-permute-start | bytes 3145736 | tf_op jit(solution)/shard_map/ppermute | solution.py:347
  503.0 44.5 %collective-permute-start.22 = (f32[128,2048]{1,0:T(8,128)}, f32[128,2048]{1,0:T(8,128)}, u32[]{:S(2)}, u32[]{:S(2)}) collective-permute-start(f32[128,2048]{1,0:T(8,128)} %get-tuple-element.201), channel_id=1, source_target_pairs={{0,8},{8,0},{1,9},{9,1},{2,10},{10,2},{3,11},{11,3},{4,12},{12,4},... | collective-permute-start | bytes 3145736 | tf_op jit(solution)/shard_map/ppermute | solution.py:399
  521.9 27.2 %collective-permute-start.23 = (f32[1024,256]{1,0:T(8,128)}, f32[1024,256]{1,0:T(8,128)}, u32[]{:S(2)}, u32[]{:S(2)}) collective-permute-start(f32[1024,256]{1,0:T(8,128)} %get-tuple-element.204), channel_id=1, source_target_pairs={{0,8},{8,0},{1,9},{9,1},{2,10},{10,2},{3,11},{11,3},{4,12},{12,4},... | collective-permute-start | bytes 3145736 | tf_op jit(solution)/shard_map/ppermute | solution.py:399
  531.9 17.9 %collective-permute-start.26 = (f32[64,1024]{1,0:T(8,128)}, f32[64,1024]{1,0:T(8,128)}, u32[]{:S(2)}, u32[]{:S(2)}) collective-permute-start(f32[64,1024]{1,0:T(8,128)} %get-tuple-element.175), channel_id=1, source_target_pairs={{0,4},{1,5},{2,6},{3,7},{4,0},{5,1},{6,2},{7,3},{8,12},{9,13},{10,... | collective-permute-start | bytes 786440 | tf_op jit(solution)/shard_map/ppermute | solution.py:347
  540.4 31.0 %collective-permute-start.27 = (f32[64,1024]{1,0:T(8,128)}, f32[64,1024]{1,0:T(8,128)}, u32[]{:S(2)}, u32[]{:S(2)}) collective-permute-start(f32[64,1024]{1,0:T(8,128)} %get-tuple-element.176), channel_id=1, source_target_pairs={{0,2},{1,3},{2,0},{3,1},{4,6},{5,7},{6,4},{7,5},{8,10},{9,11},{10,... | collective-permute-start | bytes 786440 | tf_op jit(solution)/shard_map/ppermute | solution.py:347
  541.7 31.1 %collective-permute-start.28 = (f32[64,1536]{1,0:T(8,128)}, f32[64,1536]{1,0:T(8,128)S(1)}, u32[]{:S(2)}, u32[]{:S(2)}) collective-permute-start(f32[64,1536]{1,0:T(8,128)} %get-tuple-element.177), channel_id=1, source_target_pairs={{0,4},{1,5},{2,6},{3,7},{4,0},{5,1},{6,2},{7,3},{8,12},{9,13},{10,... | collective-permute-start | bytes 1179656 | tf_op jit(solution)/shard_map/ppermute | solution.py:347
  547.5 46.9 %collective-permute-start.43 = (f32[1024,256]{1,0:T(8,128)}, f32[1024,256]{1,0:T(8,128)}, u32[]{:S(2)}, u32[]{:S(2)}) collective-permute-start(f32[1024,256]{1,0:T(8,128)} %get-tuple-element.206), channel_id=1, source_target_pairs={{0,8},{8,0},{1,9},{9,1},{2,10},{10,2},{3,11},{11,3},{4,12},{12,4},... | collective-permute-start | bytes 3145736 | tf_op jit(solution)/shard_map/ppermute | solution.py:399
  549.1 32.6 %collective-permute-start.24 = (f32[2,64,1536]{2,1,0:T(8,128)}, f32[2,64,1536]{2,1,0:T(8,128)S(1)}, u32[]{:S(2)}, u32[]{:S(2)}) collective-permute-start(f32[2,64,1536]{2,1,0:T(8,128)} %get-tuple-element.173), channel_id=1, source_target_pairs={{0,2},{1,3},{2,0},{3,1},{4,6},{5,7},{6,4},{7,5},{8,10},{9,11},{10,... | collective-permute-start | bytes 2359304 | tf_op jit(solution)/shard_map/ppermute | solution.py:347
  549.8 32.7 %collective-permute-start.25 = (f32[2,64,1536]{2,1,0:T(8,128)}, f32[2,64,1536]{2,1,0:T(8,128)S(1)}, u32[]{:S(2)}, u32[]{:S(2)}) collective-permute-start(f32[2,64,1536]{2,1,0:T(8,128)} %get-tuple-element.174), channel_id=1, source_target_pairs={{0,4},{1,5},{2,6},{3,7},{4,0},{5,1},{6,2},{7,3},{8,12},{9,13},{10,... | collective-permute-start | bytes 2359304 | tf_op jit(solution)/shard_map/ppermute | solution.py:347
  550.9 20.5 %copy-start.25 = (f32[6,1024]{1,0:T(8,128)S(1)}, f32[6,1024]{1,0:T(8,128)}, u32[]{:S(2)}) copy-start(f32[6,1024]{1,0:T(8,128)} %slice.112) | copy-start | bytes 73732
  550.9 23.4 %copy-start.26 = (f32[8192]{0:T(1024)S(1)}, f32[8192]{0:T(1024)}, u32[]{:S(2)}) copy-start(f32[8192]{0:T(1024)} %pad.13.clone) | copy-start | bytes 98308
  550.9 23.4 %copy-start.27 = (f32[8,384]{1,0:T(8,128)S(1)}, f32[8,384]{1,0:T(8,128)}, u32[]{:S(2)}) copy-start(f32[8,384]{1,0:T(8,128)} %reshape_reshape.10) | copy-start | bytes 36868
  571.4 10.3 %collective-permute-start.29 = (f32[64,1536]{1,0:T(8,128)}, f32[64,1536]{1,0:T(8,128)S(1)}, u32[]{:S(2)}, u32[]{:S(2)}) collective-permute-start(f32[64,1536]{1,0:T(8,128)} %get-tuple-element.178), channel_id=1, source_target_pairs={{0,2},{1,3},{2,0},{3,1},{4,6},{5,7},{6,4},{7,5},{8,10},{9,11},{10,... | collective-permute-start | bytes 1179656 | tf_op jit(solution)/shard_map/ppermute | solution.py:347
  572.7 24.2 %collective-permute-start.42 = (f32[128,2048]{1,0:T(8,128)}, f32[128,2048]{1,0:T(8,128)}, u32[]{:S(2)}, u32[]{:S(2)}) collective-permute-start(f32[128,2048]{1,0:T(8,128)} %get-tuple-element.203), channel_id=1, source_target_pairs={{0,8},{8,0},{1,9},{9,1},{2,10},{10,2},{3,11},{11,3},{4,12},{12,4},... | collective-permute-start | bytes 3145736 | tf_op jit(solution)/shard_map/ppermute | solution.py:399
  590.3 11.6 %collective-permute-start.32 = (f32[64,1536]{1,0:T(8,128)}, f32[64,1536]{1,0:T(8,128)S(1)}, u32[]{:S(2)}, u32[]{:S(2)}) collective-permute-start(f32[64,1536]{1,0:T(8,128)} %get-tuple-element.188), channel_id=1, source_target_pairs={{0,4},{1,5},{2,6},{3,7},{4,0},{5,1},{6,2},{7,3},{8,12},{9,13},{10,... | collective-permute-start | bytes 1179656 | tf_op jit(solution)/shard_map/ppermute | solution.py:347
  590.5 11.4 %collective-permute-start.33 = (f32[64,1536]{1,0:T(8,128)}, f32[64,1536]{1,0:T(8,128)S(1)}, u32[]{:S(2)}, u32[]{:S(2)}) collective-permute-start(f32[64,1536]{1,0:T(8,128)} %get-tuple-element.189), channel_id=1, source_target_pairs={{0,2},{1,3},{2,0},{3,1},{4,6},{5,7},{6,4},{7,5},{8,10},{9,11},{10,... | collective-permute-start | bytes 1179656 | tf_op jit(solution)/shard_map/ppermute | solution.py:347
  591.4 10.5 %collective-permute-start.34 = (f32[2,2,64,128]{3,2,1,0:T(8,128)S(1)}, f32[2,2,64,128]{3,2,1,0:T(8,128)S(1)}, u32[]{:S(2)}, u32[]{:S(2)}) collective-permute-start(f32[2,2,64,128]{3,2,1,0:T(8,128)S(1)} %dynamic-slice_bitcast_fusion.6), channel_id=1, source_target_pairs={{0,1},{1,0},{2,3},{3,2},{4,5},{5,4},{6,7},{7,6},{8,9},{9,8},{10,11... | collective-permute-start | bytes 393224 | tf_op jit(solution)/shard_map/ppermute | solution.py:347
  599.9 40.1 %collective-permute-start.41 = (f32[64,1024]{1,0:T(8,128)}, f32[64,1024]{1,0:T(8,128)}, u32[]{:S(2)}, u32[]{:S(2)}) collective-permute-start(f32[64,1024]{1,0:T(8,128)} %get-tuple-element.200), channel_id=1, source_target_pairs={{0,8},{8,0},{1,9},{9,1},{2,10},{10,2},{3,11},{11,3},{4,12},{12,4},... | collective-permute-start | bytes 786440 | tf_op jit(solution)/shard_map/ppermute | solution.py:399
  601.0 40.1 %collective-permute-start.40 = (f32[64,1024]{1,0:T(8,128)}, f32[64,1024]{1,0:T(8,128)}, u32[]{:S(2)}, u32[]{:S(2)}) collective-permute-start(f32[64,1024]{1,0:T(8,128)} %get-tuple-element.199), channel_id=1, source_target_pairs={{0,8},{8,0},{1,9},{9,1},{2,10},{10,2},{3,11},{11,3},{4,12},{12,4},... | collective-permute-start | bytes 786440 | tf_op jit(solution)/shard_map/ppermute | solution.py:399
  608.0 4.9 collective-permute-start.37
  610.9 38.3 %collective-permute-start.31 = (f32[64,1536]{1,0:T(8,128)}, f32[64,1536]{1,0:T(8,128)}, u32[]{:S(2)}, u32[]{:S(2)}) collective-permute-start(f32[64,1536]{1,0:T(8,128)} %get-tuple-element.187), channel_id=1, source_target_pairs={{0,8},{8,0},{1,9},{9,1},{2,10},{10,2},{3,11},{11,3},{4,12},{12,4},... | collective-permute-start | bytes 1179656 | tf_op jit(solution)/shard_map/ppermute | solution.py:399
  612.2 38.1 %collective-permute-start.30 = (f32[64,1536]{1,0:T(8,128)S(1)}, f32[64,1536]{1,0:T(8,128)}, u32[]{:S(2)}, u32[]{:S(2)}) collective-permute-start(f32[64,1536]{1,0:T(8,128)S(1)} %copy-done.18), channel_id=1, source_target_pairs={{0,8},{8,0},{1,9},{9,1},{2,10},{10,2},{3,11},{11,3},{4,12},{12,4},... | collective-permute-start | bytes 1179656 | tf_op jit(solution)/shard_map/ppermute | solution.py:399
  616.3 25.9 %collective-permute-start.38 = (f32[64,128]{1,0:T(8,128)}, f32[64,128]{1,0:T(8,128)}, u32[]{:S(2)}, u32[]{:S(2)}) collective-permute-start(f32[64,128]{1,0:T(8,128)} %moves.18), channel_id=1, source_target_pairs={{0,4},{1,5},{2,6},{3,7},{4,0},{5,1},{6,2},{7,3},{8,12},{9,13},{10,... | collective-permute-start | bytes 98312 | tf_op jit(solution)/shard_map/ppermute | solution.py:347
  645.6 5.8 collective-permute-start.39
  647.1 12.0 %collective-permute-start.36 = (f32[64,1536]{1,0:T(8,128)S(1)}, f32[64,1536]{1,0:T(8,128)S(1)}, u32[]{:S(2)}, u32[]{:S(2)}) collective-permute-start(f32[64,1536]{1,0:T(8,128)S(1)} %copy-done.20), channel_id=1, source_target_pairs={{0,8},{8,0},{1,9},{9,1},{2,10},{10,2},{3,11},{11,3},{4,12},{12,4},... | collective-permute-start | bytes 1179656 | tf_op jit(solution)/shard_map/ppermute | solution.py:399
  648.4 17.0 %collective-permute-start.35 = (f32[64,1536]{1,0:T(8,128)S(1)}, f32[64,1536]{1,0:T(8,128)S(1)}, u32[]{:S(2)}, u32[]{:S(2)}) collective-permute-start(f32[64,1536]{1,0:T(8,128)S(1)} %copy-done.19), channel_id=1, source_target_pairs={{0,8},{8,0},{1,9},{9,1},{2,10},{10,2},{3,11},{11,3},{4,12},{12,4},... | collective-permute-start | bytes 1179656 | tf_op jit(solution)/shard_map/ppermute | solution.py:399
  (31 other events, 114.0 us)
Sparse Core Ops, SparseCore 0:
  11.6 53.4 all-gather.6
  67.5 50.5 all-gather.8
  120.6 50.4 all-gather.10

commit v2 on v1

--- a/solution.py
+++ b/solution.py
@@ -447,6 +447,59 @@
             for i in range(pieces)]
 
 
+def finish_mlp_kernel(up0, up0_got, up1, up1_got, down0, down0_got, down1, down1_got, up_ref, down_ref):
+    up_ref[:, :FC] = up0[...] + up0_got[...]
+    up_ref[:, FC:] = up1[...] + up1_got[...]
+    down_ref[:FC, :] = (down0[...] + down0_got[...]).T
+    down_ref[FC:, :] = (down1[...] + down1_got[...]).T
+
+
+def finish_mlp(mlp):
+    rows = D // NS
+    ups = [val for pair in mlp for val in (pair[0].part, pair[0].got4)]
+    downs = [val for pair in mlp for val in (pair[1].part, pair[1].got4)]
+    return pl.pallas_call(
+        finish_mlp_kernel,
+        grid=(NS,),
+        in_specs=[pl.BlockSpec((rows, FC), lambda s: (0, s))] * 4 + [pl.BlockSpec((rows, FC), lambda s: (s, 0))] * 4,
+        out_specs=[pl.BlockSpec((rows, 2 * FC), lambda s: (0, s)), pl.BlockSpec((2 * FC, rows), lambda s: (0, s))],
+        out_shape=[jax.ShapeDtypeStruct((rows, FF), F32), jax.ShapeDtypeStruct((FF // NS, D), F32)],
+        compiler_params=pltpu.CompilerParams(dimension_semantics=("arbitrary",)),
+        cost_estimate=pl.CostEstimate(flops=1_000_000_000, bytes_accessed=12_000_000, transcendentals=0),
+        name="finish_mlp",
+    )(*ups, *downs)
+
+
+def finish_attn_kernel(*refs):
+    out_ref, qkv_ref = refs[12:]
+    cut = D // NS // 2
+    for i in range(2):
+        rows = slice(i * cut, (i + 1) * cut)
+        for half in range(2):
+            at = 4 + 4 * half + 2 * i
+            qkv_ref[rows, half * HALF:(half + 1) * HALF] = refs[at][...] + refs[at + 1][...]
+
+    @pl.when(pl.program_id(0) == 0)
+    def _():
+        for i in range(2):
+            out_ref[i * cut:(i + 1) * cut, :] = refs[2 * i][...] + refs[2 * i + 1][...]
+
+
+def finish_attn(out_red, qkv0, qkv1):
+    rows = D // NS
+    vals = [val for r in (*out_red, *qkv0, *qkv1) for val in (r.part, r.got4)]
+    return pl.pallas_call(
+        finish_attn_kernel,
+        grid=(3,),
+        in_specs=[pl.BlockSpec((rows // 2, D), lambda s: (0, 0))] * 4 + [pl.BlockSpec((rows // 2, HALF), lambda s: (0, s))] * 8,
+        out_specs=[pl.BlockSpec((rows, D), lambda s: (0, 0)), pl.BlockSpec((rows, D), lambda s: (0, s))],
+        out_shape=[jax.ShapeDtypeStruct((rows, D), F32), jax.ShapeDtypeStruct((rows, 3 * D), F32)],
+        compiler_params=pltpu.CompilerParams(dimension_semantics=("arbitrary",)),
+        cost_estimate=pl.CostEstimate(flops=1_000_000_000, bytes_accessed=6_000_000, transcendentals=0),
+        name="finish_attn",
+    )(*vals)
+
+
 def row_major(val):
     return with_layout_constraint(val, Layout(major_to_minor=tuple(range(val.ndim))))
 
@@ -547,16 +600,11 @@
         advance((), (qkv1, "rep"), (small_red, "near"))
         advance((), (small_red, "far"))
         advance((), (small_red, "rep"))
-        whole = lambda group: jnp.concatenate([r.result() for r in group], axis=0)
-        grad_w_out = whole(out_red)
-        grad_w_qkv = from_half(jnp.concatenate([whole(qkv0), whole(qkv1)], axis=1))
-        grad_up = [pair[0].result().reshape(D // NS, NS, FC) for pair in mlp]
-        grad_down = [pair[1].result().T for pair in mlp]
-
+        grad_up, grad_down = finish_mlp(mlp)
+        grad_w_out, grad_w_qkv = finish_attn(out_red, qkv0, qkv1)
         mine = small_red[0].result().reshape(-1)
-        return (z, dx, grad_w_qkv, mine[:nq], grad_w_out,
-                jnp.stack(grad_up, axis=2).reshape(D // NS, FF), mine[nq:nq + nu],
-                jnp.concatenate(grad_down, axis=0), mine[nq + nu:nq + nu + D].reshape(8, D // NS))
+        return (z, dx, grad_w_qkv, mine[:nq], grad_w_out, grad_up, mine[nq:nq + nu], grad_down,
+                mine[nq + nu:nq + nu + D].reshape(8, D // NS))
 
     return jax.shard_map(layer_step, mesh=mesh, in_specs=(batch_spec, batch_spec) + param_specs,
                          out_specs=(batch_spec, batch_spec) + param_specs, check_vma=False)

time: 681 us -> 690 us (1.013)
  waiting for transfers between devices: 93.1 us -> 121 us
  other arithmetic: 36.1 us -> 19.4 us
  local copies, waits for them, and re-layouts: 101 us -> 86.4 us
  Pallas kernels: 324 us -> 336 us
    ppermute x11, waiting for transfers between devices: 12.3 us -> 29.4 us  [start(): self.got4 = lax.ppermute(value, 'rep', [(0, 1), (1, 0)])]
    pallas_call x0 -> x2, Pallas kernels: none -> 12.3 us  [the longest x1 7.74 us: finish_mlp(): pl.pallas_call(finish_mlp_kernel, grid=(NS,), in_specs=[pl.BlockSpec((row...]
    ppermute x33, waiting for transfers between devices: 80.7 us -> 91.1 us  [exchange(): return lax.ppermute(val, 'fsdp', [(i, i ^ bit) for i in range(NS)])]
    add x9 -> x1, other arithmetic: 7.8 us -> 0.76 us  [result(): return self.part + self.got4]
    unnamed x116 -> x130, local copies, waits for them, and re-layouts: 44.5 us -> 40 us
  transfers between devices with their start and end apart: 47 -> 47, of which waited for: 9 -> 19; matrix products, arithmetic and copies ran while one was open for 26% -> 21% of each run, Pallas kernels for 48% -> 49%
where the time goes in v2:
time: 690 us; the launch traced here: 683 us
  Pallas kernels  336 us (49%)
  waiting for transfers between devices  121 us (18%)
  local copies, waits for them, and re-layouts  86.4 us (13%)
  matrix products  55.1 us (8%)
  starting transfers between devices  39.5 us (6%)
  other arithmetic  19.4 us (3%)
  between operations  14.8 us (2%)
  blocking collectives  11.4 us (2%)
    pallas_call x2, Pallas kernels, mlp_chunk(): pl.pallas_call(mlp_kernel, grid=(cols // BLK,), in_specs=[whole((T, D)),...  138 us
    ppermute x33, waiting for transfers between devices, exchange(): return lax.ppermute(val, 'fsdp', [(i, i ^ bit) for i in range(NS)])  91.1 us
    pallas_call x2, Pallas kernels, attn_backward(): pl.pallas_call(attn_bwd_kernel, grid=(T // ROWS,), in_specs=[spec(3 * hal...  67.1 us
    pallas_call x10, Pallas kernels, advance(): pl.pallas_call(functools.partial(moves_kernel, [len(ins) for ins, _, _ in...  57.7 us
    unnamed x130, local copies, waits for them, and re-layouts  40 us
    ppermute x11, waiting for transfers between devices, start(): self.got4 = lax.ppermute(value, 'rep', [(0, 1), (1, 0)])  29.4 us
    ppermute x33, starting transfers between devices, exchange(): return lax.ppermute(val, 'fsdp', [(i, i ^ bit) for i in range(NS)])  25.4 us
    dot_general x3, matrix products, dot_tn(): lax.dot_general(a, b, (((0,), (0,)), ((), ())), preferred_element_type=F32)  25.2 us
  transfers between devices with their start and end apart: 47, of which 19 were waited for; matrix products, arithmetic and copies ran while one was open for 21% of the time, Pallas kernels for 49%

profile of v2, /device:TPU:0, one launch (start us, length us, event | category | flops | bytes accessed | tf_op | source)
XLA Modules:
  0.0 683.3 jit_solution(1834850231882845920)
XLA Ops:
  8.3 1.8 copy.52
  11.6 1.9 convert.36
  14.7 5.1 slice_reduce_fusion
  21.8 1.6 copy.70
  23.5 2.0 maximum_maximum_fusion.1
  25.6 11.4 %all-gather.2 = bf16[8,1,1920]{2,1,0:T(2,128)(2,1)S(1)} all-gather(bf16[1,1,1920]{2,1,0:T(2,128)(2,1)S(1)} %maximum_bitcast_fusion.2), channel_id=1, replica_groups=mesh['rep'=2,'fsdp'=8] {'fsdp'}, dimensions={0}, use_global_device_ids=true | all-gather | bytes 34560 | tf_op jit(solution)/shard_map/all_gather | solution.py:536
  37.1 3.7 copy.50
  40.8 3.2 reshape.194.x_ref
  44.0 6.8 copy.56
  50.8 4.6 reshape.198.g_ref
  55.5 4.6 multiply_convert_fusion.g_ref
  60.1 5.4 copy.58
  68.4 16.4 %add_convert_fusion.q_ref.k_ref.v_ref = bf16[1600,3072]{1,0:T(8,128)(2,1)} fusion(f32[3072]{0:T(1024)S(1)} %add.81, bf16[1024,4096]{1,0:T(8,128)(2,1)} %all-gather.7.cloned.1.call-done.w_ref, bf16[1600,1024]{1,0:T(8,128)(2,1)S(1)} %reshape.194.x_ref, f32[1024]{0:T(1024)S(1)} %bitcast.195, f32[1024]{0:T(1024)S(1)} %bitcast.198, f32[1600]{0:T(1024)S(1)} %add_rsqrt_fusion.1, ...), kind=kOutput, calls=%fused_computation | convolution fusion | flops 10085990400 | bytes 19431936 | tf_op jit(solution)/shard_map/dot_general | solution.py:38
  84.7 20.8 %attn_fwd.1 = bf16[1600,1024]{1,0:T(8,128)(2,1)} custom-call(bf16[1600,3072]{1,0:T(8,128)(2,1)} %add_convert_fusion.q_ref.k_ref.v_ref, bf16[1600,3072]{1,0:T(8,128)(2,1)} %add_convert_fusion.q_ref.k_ref.v_ref, bf16[1600,3072]{1,0:T(8,128)(2,1)} %add_convert_fusion.q_ref.k_ref.v_ref), custom_call_target="tpu_custom_call" | custom-call | flops 8000000000 | bytes 13000000 | tf_op jit(solution)/shard_map/attn_fwd/pallas_call | solution.py:156
  105.6 7.0 %fusion.9 = (f32[1600]{0:T(1024)S(1)}, f32[1600,1024]{1,0:T(8,128)S(1)}) fusion(f32[1024]{0:T(1024)S(1)} %bitcast.182, bf16[1600,1024]{1,0:T(8,128)(2,1)S(1)} %reshape.194.x_ref, f32[1024]{0:T(1024)S(1)} %bitcast.201, bf16[1600,1024]{1,0:T(8,128)(2,1)} %attn_fwd.1, bf16[1024,4096]{1,0:T(8,128)(2,1)} %all-gather.7.cloned.1.call-done.w_ref), kind=kOutput, calls=%fused_computation.18 | convolution fusion | flops 3363633664 | bytes 15218944 | tf_op jit(solution)/shard_map/dot_general | solution.py:38
  115.3 3.1 add_convert_fusion.1.h_ref
  118.4 5.5 copy.57
  123.9 69.6 %mlp_fwd_bwd.2 = (f32[1600,1024]{1,0:T(8,128)}, f32[1600,1024]{1,0:T(8,128)}, f32[4,128,2048]{2,1,0:T(8,128)}, f32[4,128,2048]{2,1,0:T(8,128)}, f32[4,1024,256]{...) custom-call(bf16[1600,1024]{1,0:T(8,128)(2,1)} %add_convert_fusion.1.h_ref, ...), custom_call_target="tpu_custom_call" | custom-call | flops 40265318400 | bytes 60000000 | tf_op jit(solution)/shard_map/mlp_fwd_bwd/pallas_call | solution.py:236
  194.1 68.6 %mlp_fwd_bwd.3 = (f32[1600,1024]{1,0:T(8,128)}, f32[1600,1024]{1,0:T(8,128)}, f32[4,128,2048]{2,1,0:T(8,128)}, f32[4,128,2048]{2,1,0:T(8,128)}, f32[4,1024,256]{...) custom-call(bf16[1600,1024]{1,0:T(8,128)(2,1)} %add_convert_fusion.1.h_ref, ...), custom_call_target="tpu_custom_call" | custom-call | flops 40265318400 | bytes 60000000 | tf_op jit(solution)/shard_map/mlp_fwd_bwd/pallas_call | solution.py:236
  263.9 6.4 moves.10
  273.0 20.2 %post_mlp.1 = (bf16[1600,1024]{1,0:T(8,128)(2,1)}, f32[1600,1024]{1,0:T(8,128)}, bf16[1600,1024]{1,0:T(8,128)(2,1)}, f32[8,1024]{1,0:T(8,128)}) custom-call(f32[1600,1024]{1,0:T(8,128)} %get-tuple-element.122.m0_ref, f32[1600,1024]{1,0:T(8,128)} %get-tuple-element.123.m1_ref, f32[1600,1024]{1,0:T(8,128)} %get-tuple-element.124.d0_ref, ...), custom_call_target="tpu_custom_call" | custom-call | flops 5000000000 | bytes 56000000 | tf_op jit(solution)/shard_map/post_mlp/pallas_call | solution.py:285
  293.2 6.9 %fusion.19 = f32[1024,1024]{1,0:T(8,128)S(1)} fusion(bf16[1600,1024]{1,0:T(8,128)(2,1)} %attn_fwd.1, bf16[1600,1024]{1,0:T(8,128)(2,1)} %get-tuple-element.126), kind=kOutput, calls=%fused_computation.64 | convolution fusion | flops 3355443200 | bytes 10747904 | tf_op jit(solution)/shard_map/dot_general | solution.py:46
  304.8 6.5 convolution_convert_fusion.g_ref
  311.4 6.9 %collective-permute-done.2.refs_2_.refs_6_ = f32[2,128,2048]{2,1,0:T(8,128)S(1)} collective-permute-done((f32[2,128,2048]{2,1,0:T(8,128)}, f32[2,128,2048]{2,1,0:T(8,128)S(1)}, u32[]{:S(2)}, u32[]{:S(2)}) %collective-permute-start.2) | collective-permute-done | bytes 2097184 | tf_op jit(solution)/shard_map/ppermute | solution.py:347
  319.6 8.6 %moves.11 = (f32[128,2048]{1,0:T(8,128)}, f32[1024,256]{1,0:T(8,128)}, f32[2,128,2048]{2,1,0:T(8,128)}, f32[2,1024,256]{2,1,0:T(8,128)}) custom-call(s32[3]{0:T(128)} %pad_add_fusion.idx_ref, f32[2,2,1,128,2048]{4,3,2,1,0:T(8,128)} %bitcast.142, f32[2,2,128,2048]{3,2,1,0:T(8,128)} %collective-permute-done.refs_1_.refs_5_, f32[2,128,2048]{2,1,0:T(8,128)} %copy-done.8, ...), custom_call_target="tpu_custom_call" | custom-call | flops 1000000000 | bytes 10000000 | tf_op jit(solution)/shard_map/moves/pallas_call | solution.py:424
  328.3 33.6 %attn_bwd.2 = (bf16[1600,1536]{1,0:T(8,128)(2,1)}, f32[4,1,1536]{2,1,0:T(1,128)}) custom-call(bf16[1600,3072]{1,0:T(8,128)(2,1)} %add_convert_fusion.q_ref.k_ref.v_ref, bf16[1600,3072]{1,0:T(8,128)(2,1)} %add_convert_fusion.q_ref.k_ref.v_ref, bf16[1600,3072]{1,0:T(8,128)(2,1)} %add_convert_fusion.q_ref.k_ref.v_ref, ...), custom_call_target="tpu_custom_call" | custom-call | flops 16000000000 | bytes 12000000 | tf_op jit(solution)/shard_map/attn_bwd/pallas_call | solution.py:170
  365.5 9.1 %fusion.12 = f32[1024,1536]{1,0:T(8,128)S(1)} fusion(bf16[1600,1536]{1,0:T(8,128)(2,1)} %get-tuple-element.138.d0_ref, bf16[1600,1024]{1,0:T(8,128)(2,1)S(1)} %copy-done.4, f32[1024]{0:T(1024)S(1)} %bitcast.196, f32[1024]{0:T(1024)S(1)} %bitcast.199, f32[1600]{0:T(1024)S(1)} %copy-done.44, f32[1600]{0:T(1024)S(1)} %copy-done.36), kind=kOutput, calls=%fused_computation.57 | convolution fusion | flops 5042995200 | bytes 14504448 | tf_op jit(solution)/shard_map/dot_general | solution.py:46
  375.2 2.0 copy-done
  380.3 8.0 %collective-permute-done.8.refs_7_ = f32[128,2048]{1,0:T(8,128)} collective-permute-done((f32[128,2048]{1,0:T(8,128)}, f32[128,2048]{1,0:T(8,128)}, u32[]{:S(2)}, u32[]{:S(2)}) %collective-permute-start.8) | collective-permute-done | bytes 1048608 | tf_op jit(solution)/shard_map/ppermute | solution.py:347
  389.8 43.4 %collective-permute-done.9.refs_11_ = f32[1024,256]{1,0:T(8,128)} collective-permute-done((f32[1024,256]{1,0:T(8,128)S(1)}, f32[1024,256]{1,0:T(8,128)}, u32[]{:S(2)}, u32[]{:S(2)}) %collective-permute-start.9) | collective-permute-done | bytes 1048608 | tf_op jit(solution)/shard_map/ppermute | solution.py:347
  433.2 6.8 moves.12
  441.9 6.6 moves.13
  448.4 33.5 %attn_bwd.3 = (bf16[1600,1536]{1,0:T(8,128)(2,1)}, f32[4,1,1536]{2,1,0:T(1,128)}) custom-call(bf16[1600,3072]{1,0:T(8,128)(2,1)} %add_convert_fusion.q_ref.k_ref.v_ref, bf16[1600,3072]{1,0:T(8,128)(2,1)} %add_convert_fusion.q_ref.k_ref.v_ref, bf16[1600,3072]{1,0:T(8,128)(2,1)} %add_convert_fusion.q_ref.k_ref.v_ref, ...), custom_call_target="tpu_custom_call" | custom-call | flops 16000000000 | bytes 12000000 | tf_op jit(solution)/shard_map/attn_bwd/pallas_call | solution.py:170
  482.4 1.7 collective-permute-start.15
  484.4 9.1 %fusion.10 = f32[1024,1536]{1,0:T(8,128)S(1)} fusion(bf16[1600,1536]{1,0:T(8,128)(2,1)} %get-tuple-element.169.d1_ref, bf16[1600,1024]{1,0:T(8,128)(2,1)S(1)} %copy-done.4, f32[1024]{0:T(1024)S(1)} %bitcast.197, f32[1024]{0:T(1024)S(1)} %bitcast.200, f32[1600]{0:T(1024)S(1)} %copy-done.44, f32[1600]{0:T(1024)S(1)} %copy-done.36), kind=kOutput, calls=%fused_computation.56 | convolution fusion | flops 5042995200 | bytes 14504448 | tf_op jit(solution)/shard_map/dot_general | solution.py:46
  494.2 2.0 copy-done.1
  500.9 2.3 collective-permute-done.15.refs_5_.refs_20_
  503.1 1.6 collective-permute-start.22
  504.8 17.6 %collective-permute-done.18.refs_15_ = f32[128,2048]{1,0:T(8,128)} collective-permute-done((f32[128,2048]{1,0:T(8,128)}, f32[128,2048]{1,0:T(8,128)}, u32[]{:S(2)}, u32[]{:S(2)}) %collective-permute-start.18) | collective-permute-done | bytes 1048608 | tf_op jit(solution)/shard_map/ppermute | solution.py:347
  524.5 7.4 %moves.14 = (f32[64,1536]{1,0:T(8,128)}, f32[64,1536]{1,0:T(8,128)}, f32[64,1024]{1,0:T(8,128)}, f32[64,1024]{1,0:T(8,128)}, f32[128,2048]{1,0:T(8,128)}, /*index=5*/f32[1024,256]{1,0:T(8,128)}) custom-call(s32[3]{0:T(128)} %pad_add_fusion.idx_ref, f32[2,2,2,128,1536]{4,3,2,1,0:T(8,128)} %bitcast.123, ...), custom_call_target="tpu_custom_call" | custom-call | flops 1000000000 | bytes 10000000 | tf_op jit(solution)/shard_map/moves/pallas_call | solution.py:424
  531.9 1.7 collective-permute-start.26
  534.3 4.7 reshape.215
  542.8 4.6 moves.15
  550.7 19.7 %ln1_back.1 = (bf16[1600,1024]{1,0:T(8,128)(2,1)}, f32[8,1024]{1,0:T(8,128)}) custom-call(bf16[1600,1536]{1,0:T(8,128)(2,1)} %get-tuple-element.138.d0_ref, bf16[1600,1536]{1,0:T(8,128)(2,1)} %get-tuple-element.169.d1_ref, bf16[1024,4096]{1,0:T(8,128)(2,1)} %all-gather.7.cloned.1.call-done.w_ref, bf16[1600,1024]{1,0:T(8,128)(2,1)} %copy-done.3, ...), custom_call_target="tpu_custom_call" | custom-call | flops 10066329600 | bytes 30000000 | tf_op jit(solution)/shard_map/ln1_back/pallas_call | solution.py:329
  576.0 5.9 moves.16
  584.8 6.1 collective-permute-done.34.refs_3_
  592.4 4.6 moves.17
  597.9 1.6 collective-permute-start.30
  599.4 2.0 collective-permute-done.39.refs_2_
  602.1 3.6 moves.18
  606.7 5.5 copy.62
  612.9 3.4 moves.19
  617.8 1.6 collective-permute-done.43.down1_got
  619.4 7.7 %finish_mlp.1 = (f32[128,4096]{1,0:T(8,128)}, f32[512,1024]{1,0:T(8,128)}) custom-call(f32[128,2048]{1,0:T(8,128)} %get-tuple-element.207.up0, f32[128,2048]{1,0:T(8,128)} %collective-permute-done.22.up0_got, f32[128,2048]{1,0:T(8,128)} %get-tuple-element.209.up1, f32[128,2048]{1,0:T(8,128)} %collective-permute-done.42.up1_got, ...), custom_call_target="tpu_custom_call" | custom-call | flops 1000000000 | bytes 12000000 | tf_op jit(solution)/shard_map/finish_mlp/pallas_call | solution.py:461
  627.2 2.6 reshape.216
  629.8 5.7 copy.63
  635.5 1.6 collective-permute-start.31
  637.5 1.6 collective-permute-start.33
  640.3 1.6 collective-permute-start.38
  644.7 8.4 %collective-permute-done.32.refs_5_ = f32[64,1536]{1,0:T(8,128)S(1)} collective-permute-done((f32[64,1536]{1,0:T(8,128)S(1)}, f32[64,1536]{1,0:T(8,128)S(1)}, u32[]{:S(2)}, u32[]{:S(2)}) %collective-permute-start.32) | collective-permute-done | bytes 393248 | tf_op jit(solution)/shard_map/ppermute | solution.py:399
  653.1 8.4 %collective-permute-done.33.refs_7_ = f32[64,1536]{1,0:T(8,128)S(1)} collective-permute-done((f32[64,1536]{1,0:T(8,128)S(1)}, f32[64,1536]{1,0:T(8,128)S(1)}, u32[]{:S(2)}, u32[]{:S(2)}) %collective-permute-start.33) | collective-permute-done | bytes 393248 | tf_op jit(solution)/shard_map/ppermute | solution.py:399
  661.5 5.5 collective-permute-done.37.refs_9_
  667.0 4.2 collective-permute-done.38.refs_11_
  672.0 4.6 finish_attn.1
  (255 shorter events, 68.0 us)
Async XLA Ops:
  7.2 61.2 %all-gather.7.cloned.1.call-start = ((), (), s32[]{:S(2)}) async-start(), calls=%async_computation | async-start | bytes 9437184 | tf_op jit(solution)/shard_map/all_gather | solution.py:343
  11.5 112.4 %all-gather.9.cloned.1.call-start = ((), (), s32[]{:S(2)}) async-start(), calls=%async_computation.1 | async-start | bytes 9437184 | tf_op jit(solution)/shard_map/all_gather | solution.py:534
  20.7 16.5 %copy-start.9 = (bf16[32,50,1024]{2,0,1:T(8,128)(2,1)S(1)}, bf16[32,50,1024]{2,0,1:T(8,128)(2,1)}, u32[]{:S(2)}) copy-start(bf16[32,50,1024]{2,0,1:T(8,128)(2,1)} %param.9) | copy-start | bytes 9830404
  21.8 172.3 %all-gather.11.cloned.1.call-start = ((), (), s32[]{:S(2)}) async-start(), calls=%async_computation.2 | async-start | bytes 9437184 | tf_op jit(solution)/shard_map/all_gather | solution.py:534
  44.0 70.1 %copy-start.3 = (bf16[1600,1024]{1,0:T(8,128)(2,1)}, bf16[1600,1024]{1,0:T(8,128)(2,1)S(1)}, u32[]{:S(2)}) copy-start(bf16[1600,1024]{1,0:T(8,128)(2,1)S(1)} %reshape.194.x_ref) | copy-start | bytes 9830404
  55.5 12.9 %copy-start.45 = (f32[1,8,128]{2,0,1:T(1,128)}, f32[1,8,128]{2,0,1:T(1,128)S(1)}, u32[]{:S(2)}) copy-start(f32[1,8,128]{2,0,1:T(1,128)S(1)} %get-tuple-element.270) | copy-start | bytes 12292
  55.5 12.9 %copy-start.47 = (f32[1,8,128]{2,0,1:T(1,128)}, f32[1,8,128]{2,0,1:T(1,128)S(1)}, u32[]{:S(2)}) copy-start(f32[1,8,128]{2,0,1:T(1,128)S(1)} %get-tuple-element.271) | copy-start | bytes 12292
  67.3 17.5 %copy-start.35 = (f32[1600]{0:T(1024)}, f32[1600]{0:T(1024)S(1)}, u32[]{:S(2)}) copy-start(f32[1600]{0:T(1024)S(1)} %broadcast_multiply_fusion.1) | copy-start | bytes 19204
  68.3 16.4 %copy-start.43 = (f32[1600]{0:T(1024)}, f32[1600]{0:T(1024)S(1)}, u32[]{:S(2)}) copy-start(f32[1600]{0:T(1024)S(1)} %add_rsqrt_fusion.1) | copy-start | bytes 19204
  193.5 70.3 %collective-permute-start = (f32[2,2,128,2048]{3,2,1,0:T(8,128)}, f32[2,2,128,2048]{3,2,1,0:T(8,128)}, u32[]{:S(2)}, u32[]{:S(2)}) collective-permute-start(f32[2,2,128,2048]{3,2,1,0:T(8,128)} %bitcast.209), channel_id=1, source_target_pairs={{0,1},{1,0},{2,3},{3,2},{4,5},{5,4},{6,7},{7,6},{8,9},{9,8},{10,11... | collective-permute-start | bytes 12582920 | tf_op jit(solution)/shard_map/ppermute | solution.py:347
  193.8 70.1 %collective-permute-start.1 = (f32[2,2,1024,256]{3,2,1,0:T(8,128)}, f32[2,2,1024,256]{3,2,1,0:T(8,128)}, u32[]{:S(2)}, u32[]{:S(2)}) collective-permute-start(f32[2,2,1024,256]{3,2,1,0:T(8,128)} %bitcast.208), channel_id=1, source_target_pairs={{0,1},{1,0},{2,3},{3,2},{4,5},{5,4},{6,7},{7,6},{8,9},{9,8},{10,11... | collective-permute-start | bytes 12582920 | tf_op jit(solution)/shard_map/ppermute | solution.py:347
  262.7 48.7 %collective-permute-start.4 = (f32[2,2,128,2048]{3,2,1,0:T(8,128)}, f32[2,2,128,2048]{3,2,1,0:T(8,128)}, u32[]{:S(2)}, u32[]{:S(2)}) collective-permute-start(f32[2,2,128,2048]{3,2,1,0:T(8,128)} %bitcast.207), channel_id=1, source_target_pairs={{0,1},{1,0},{2,3},{3,2},{4,5},{5,4},{6,7},{7,6},{8,9},{9,8},{10,11... | collective-permute-start | bytes 12582920 | tf_op jit(solution)/shard_map/ppermute | solution.py:347
  263.0 48.4 %collective-permute-start.5 = (f32[2,2,1024,256]{3,2,1,0:T(8,128)}, f32[2,2,1024,256]{3,2,1,0:T(8,128)}, u32[]{:S(2)}, u32[]{:S(2)}) collective-permute-start(f32[2,2,1024,256]{3,2,1,0:T(8,128)} %bitcast.206), channel_id=1, source_target_pairs={{0,1},{1,0},{2,3},{3,2},{4,5},{5,4},{6,7},{7,6},{8,9},{9,8},{10,11... | collective-permute-start | bytes 12582920 | tf_op jit(solution)/shard_map/ppermute | solution.py:347
  270.3 48.0 %collective-permute-start.2 = (f32[2,128,2048]{2,1,0:T(8,128)}, f32[2,128,2048]{2,1,0:T(8,128)S(1)}, u32[]{:S(2)}, u32[]{:S(2)}) collective-permute-start(f32[2,128,2048]{2,1,0:T(8,128)} %get-tuple-element.127), channel_id=1, source_target_pairs={{0,2},{1,3},{2,0},{3,1},{4,6},{5,7},{6,4},{7,5},{8,10},{9,11},{10,... | collective-permute-start | bytes 6291464 | tf_op jit(solution)/shard_map/ppermute | solution.py:347
  271.7 47.9 %collective-permute-start.3 = (f32[2,1024,256]{2,1,0:T(8,128)}, f32[2,1024,256]{2,1,0:T(8,128)}, u32[]{:S(2)}, u32[]{:S(2)}) collective-permute-start(f32[2,1024,256]{2,1,0:T(8,128)} %get-tuple-element.128), channel_id=1, source_target_pairs={{0,4},{1,5},{2,6},{3,7},{4,0},{5,1},{6,2},{7,3},{8,12},{9,13},{10,... | collective-permute-start | bytes 6291464 | tf_op jit(solution)/shard_map/ppermute | solution.py:347
  303.2 75.3 %collective-permute-start.6 = (f32[2,2,64,1024]{3,2,1,0:T(8,128)}, f32[2,2,64,1024]{3,2,1,0:T(8,128)}, u32[]{:S(2)}, u32[]{:S(2)}) collective-permute-start(f32[2,2,64,1024]{3,2,1,0:T(8,128)} %dynamic-slice_bitcast_fusion.5), channel_id=1, source_target_pairs={{0,1},{1,0},{2,3},{3,2},{4,5},{5,4},{6,7},{7,6},{8,9},{9,8},{10,11... | collective-permute-start | bytes 3145736 | tf_op jit(solution)/shard_map/ppermute | solution.py:347
  311.4 68.4 %collective-permute-start.7 = (f32[2,2,64,1024]{3,2,1,0:T(8,128)}, f32[2,2,64,1024]{3,2,1,0:T(8,128)}, u32[]{:S(2)}, u32[]{:S(2)}) collective-permute-start(f32[2,2,64,1024]{3,2,1,0:T(8,128)} %dynamic-slice_bitcast_fusion.4), channel_id=1, source_target_pairs={{0,1},{1,0},{2,3},{3,2},{4,5},{5,4},{6,7},{7,6},{8,9},{9,8},{10,11... | collective-permute-start | bytes 3145736 | tf_op jit(solution)/shard_map/ppermute | solution.py:347
  328.2 37.2 %copy-start.4 = (bf16[1600,1024]{1,0:T(8,128)(2,1)S(1)}, bf16[1600,1024]{1,0:T(8,128)(2,1)}, u32[]{:S(2)}) copy-start(bf16[1600,1024]{1,0:T(8,128)(2,1)} %copy-done.3) | copy-start | bytes 9830404
  328.2 37.2 %copy-start.36 = (f32[1600]{0:T(1024)S(1)}, f32[1600]{0:T(1024)}, u32[]{:S(2)}) copy-start(f32[1600]{0:T(1024)} %copy-done.35) | copy-start | bytes 19204
  328.3 37.2 %copy-start.44 = (f32[1600]{0:T(1024)S(1)}, f32[1600]{0:T(1024)}, u32[]{:S(2)}) copy-start(f32[1600]{0:T(1024)} %copy-done.43) | copy-start | bytes 19204
  328.3 37.2 %copy-start.46 = (f32[1,8,128]{2,0,1:T(1,128)S(1)}, f32[1,8,128]{2,0,1:T(1,128)}, u32[]{:S(2)}) copy-start(f32[1,8,128]{2,0,1:T(1,128)} %copy-done.45) | copy-start | bytes 12292
  328.3 37.2 %copy-start.48 = (f32[1,8,128]{2,0,1:T(1,128)S(1)}, f32[1,8,128]{2,0,1:T(1,128)}, u32[]{:S(2)}) copy-start(f32[1,8,128]{2,0,1:T(1,128)} %copy-done.47) | copy-start | bytes 12292
  361.9 26.3 %collective-permute-start.8 = (f32[128,2048]{1,0:T(8,128)}, f32[128,2048]{1,0:T(8,128)}, u32[]{:S(2)}, u32[]{:S(2)}) collective-permute-start(f32[128,2048]{1,0:T(8,128)} %get-tuple-element.139), channel_id=1, source_target_pairs={{0,4},{1,5},{2,6},{3,7},{4,0},{5,1},{6,2},{7,3},{8,12},{9,13},{10,... | collective-permute-start | bytes 3145736 | tf_op jit(solution)/shard_map/ppermute | solution.py:347
  363.4 78.4 %collective-permute-start.10 = (f32[2,128,2048]{2,1,0:T(8,128)}, f32[2,128,2048]{2,1,0:T(8,128)}, u32[]{:S(2)}, u32[]{:S(2)}) collective-permute-start(f32[2,128,2048]{2,1,0:T(8,128)} %get-tuple-element.146), channel_id=1, source_target_pairs={{0,2},{1,3},{2,0},{3,1},{4,6},{5,7},{6,4},{7,5},{8,10},{9,11},{10,... | collective-permute-start | bytes 6291464 | tf_op jit(solution)/shard_map/ppermute | solution.py:347
  364.8 77.1 %collective-permute-start.11 = (f32[2,1024,256]{2,1,0:T(8,128)}, f32[2,1024,256]{2,1,0:T(8,128)}, u32[]{:S(2)}, u32[]{:S(2)}) collective-permute-start(f32[2,1024,256]{2,1,0:T(8,128)} %get-tuple-element.147), channel_id=1, source_target_pairs={{0,4},{1,5},{2,6},{3,7},{4,0},{5,1},{6,2},{7,3},{8,12},{9,13},{10,... | collective-permute-start | bytes 6291464 | tf_op jit(solution)/shard_map/ppermute | solution.py:347
  378.5 62.8 %collective-permute-start.12 = (f32[2,2,64,1536]{3,2,1,0:T(8,128)}, f32[2,2,64,1536]{3,2,1,0:T(8,128)}, u32[]{:S(2)}, u32[]{:S(2)}) collective-permute-start(f32[2,2,64,1536]{3,2,1,0:T(8,128)} %dynamic-slice_bitcast_fusion.3), channel_id=1, source_target_pairs={{0,1},{1,0},{2,3},{3,2},{4,5},{5,4},{6,7},{7,6},{8,9},{9,8},{10,11... | collective-permute-start | bytes 4718600 | tf_op jit(solution)/shard_map/ppermute | solution.py:347
  379.8 62.1 %collective-permute-start.13 = (f32[2,2,64,1536]{3,2,1,0:T(8,128)}, f32[2,2,64,1536]{3,2,1,0:T(8,128)}, u32[]{:S(2)}, u32[]{:S(2)}) collective-permute-start(f32[2,2,64,1536]{3,2,1,0:T(8,128)} %dynamic-slice_bitcast_fusion.2), channel_id=1, source_target_pairs={{0,1},{1,0},{2,3},{3,2},{4,5},{5,4},{6,7},{7,6},{8,9},{9,8},{10,11... | collective-permute-start | bytes 4718600 | tf_op jit(solution)/shard_map/ppermute | solution.py:347
  388.3 44.9 %collective-permute-start.9 = (f32[1024,256]{1,0:T(8,128)S(1)}, f32[1024,256]{1,0:T(8,128)}, u32[]{:S(2)}, u32[]{:S(2)}) collective-permute-start(f32[1024,256]{1,0:T(8,128)S(1)} %copy-done.54), channel_id=1, source_target_pairs={{0,2},{1,3},{2,0},{3,1},{4,6},{5,7},{6,4},{7,5},{8,10},{9,11},{10,... | collective-permute-start | bytes 3145736 | tf_op jit(solution)/shard_map/ppermute | solution.py:347
  440.0 57.6 %collective-permute-start.16 = (f32[2,64,1024]{2,1,0:T(8,128)}, f32[2,64,1024]{2,1,0:T(8,128)}, u32[]{:S(2)}, u32[]{:S(2)}) collective-permute-start(f32[2,64,1024]{2,1,0:T(8,128)} %get-tuple-element.156), channel_id=1, source_target_pairs={{0,2},{1,3},{2,0},{3,1},{4,6},{5,7},{6,4},{7,5},{8,10},{9,11},{10,... | collective-permute-start | bytes 1572872 | tf_op jit(solution)/shard_map/ppermute | solution.py:347
  441.3 57.5 %collective-permute-start.17 = (f32[2,64,1024]{2,1,0:T(8,128)}, f32[2,64,1024]{2,1,0:T(8,128)}, u32[]{:S(2)}, u32[]{:S(2)}) collective-permute-start(f32[2,64,1024]{2,1,0:T(8,128)} %get-tuple-element.157), channel_id=1, source_target_pairs={{0,4},{1,5},{2,6},{3,7},{4,0},{5,1},{6,2},{7,3},{8,12},{9,13},{10,... | collective-permute-start | bytes 1572872 | tf_op jit(solution)/shard_map/ppermute | solution.py:347
  481.9 17.7 %collective-permute-start.14 = (f32[2,64,1536]{2,1,0:T(8,128)}, f32[2,64,1536]{2,1,0:T(8,128)}, u32[]{:S(2)}, u32[]{:S(2)}) collective-permute-start(f32[2,64,1536]{2,1,0:T(8,128)} %get-tuple-element.154), channel_id=1, source_target_pairs={{0,2},{1,3},{2,0},{3,1},{4,6},{5,7},{6,4},{7,5},{8,10},{9,11},{10,... | collective-permute-start | bytes 2359304 | tf_op jit(solution)/shard_map/ppermute | solution.py:347
  482.4 20.7 %collective-permute-start.15 = (f32[2,64,1536]{2,1,0:T(8,128)}, f32[2,64,1536]{2,1,0:T(8,128)}, u32[]{:S(2)}, u32[]{:S(2)}) collective-permute-start(f32[2,64,1536]{2,1,0:T(8,128)} %get-tuple-element.155), channel_id=1, source_target_pairs={{0,4},{1,5},{2,6},{3,7},{4,0},{5,1},{6,2},{7,3},{8,12},{9,13},{10,... | collective-permute-start | bytes 2359304 | tf_op jit(solution)/shard_map/ppermute | solution.py:347
  484.1 38.2 %collective-permute-start.18 = (f32[128,2048]{1,0:T(8,128)}, f32[128,2048]{1,0:T(8,128)}, u32[]{:S(2)}, u32[]{:S(2)}) collective-permute-start(f32[128,2048]{1,0:T(8,128)} %get-tuple-element.158), channel_id=1, source_target_pairs={{0,4},{1,5},{2,6},{3,7},{4,0},{5,1},{6,2},{7,3},{8,12},{9,13},{10,... | collective-permute-start | bytes 3145736 | tf_op jit(solution)/shard_map/ppermute | solution.py:347
  497.5 42.8 %collective-permute-start.20 = (f32[2,2,64,1536]{3,2,1,0:T(8,128)}, f32[2,2,64,1536]{3,2,1,0:T(8,128)S(1)}, u32[]{:S(2)}, u32[]{:S(2)}) collective-permute-start(f32[2,2,64,1536]{3,2,1,0:T(8,128)} %dynamic-slice_bitcast_fusion.1), channel_id=1, source_target_pairs={{0,1},{1,0},{2,3},{3,2},{4,5},{5,4},{6,7},{7,6},{8,9},{9,8},{10,11... | collective-permute-start | bytes 4718600 | tf_op jit(solution)/shard_map/ppermute | solution.py:347
  498.8 35.5 %copy-start.42 = (f32[1,2048]{1,0:T(1,128)S(1)}, f32[1,2048]{1,0:T(1,128)}, u32[]{:S(2)}) copy-start(f32[1,2048]{1,0:T(1,128)} %get-tuple-element.199) | copy-start | bytes 24580
  498.8 35.5 %copy-start.41 = (f32[1,2048]{1,0:T(1,128)S(1)}, f32[1,2048]{1,0:T(1,128)}, u32[]{:S(2)}) copy-start(f32[1,2048]{1,0:T(1,128)} %get-tuple-element.198) | copy-start | bytes 24580
  498.8 42.9 %collective-permute-start.21 = (f32[2,2,64,1536]{3,2,1,0:T(8,128)}, f32[2,2,64,1536]{3,2,1,0:T(8,128)S(1)}, u32[]{:S(2)}, u32[]{:S(2)}) collective-permute-start(f32[2,2,64,1536]{3,2,1,0:T(8,128)} %dynamic-slice_bitcast_fusion), channel_id=1, source_target_pairs={{0,1},{1,0},{2,3},{3,2},{4,5},{5,4},{6,7},{7,6},{8,9},{9,8},{10,11... | collective-permute-start | bytes 4718600 | tf_op jit(solution)/shard_map/ppermute | solution.py:347
  499.6 24.9 %collective-permute-start.19 = (f32[1024,256]{1,0:T(8,128)S(1)}, f32[1024,256]{1,0:T(8,128)}, u32[]{:S(2)}, u32[]{:S(2)}) collective-permute-start(f32[1024,256]{1,0:T(8,128)S(1)} %copy-done.53), channel_id=1, source_target_pairs={{0,2},{1,3},{2,0},{3,1},{4,6},{5,7},{6,4},{7,5},{8,10},{9,11},{10,... | collective-permute-start | bytes 3145736 | tf_op jit(solution)/shard_map/ppermute | solution.py:347
  503.1 44.3 %collective-permute-start.22 = (f32[128,2048]{1,0:T(8,128)}, f32[128,2048]{1,0:T(8,128)}, u32[]{:S(2)}, u32[]{:S(2)}) collective-permute-start(f32[128,2048]{1,0:T(8,128)} %get-tuple-element.207.up0), channel_id=1, source_target_pairs={{0,8},{8,0},{1,9},{9,1},{2,10},{10,2},{3,11},{11,3},{4,12},{12,4},... | collective-permute-start | bytes 3145736 | tf_op jit(solution)/shard_map/ppermute | solution.py:399
  522.3 26.1 %collective-permute-start.23 = (f32[1024,256]{1,0:T(8,128)}, f32[1024,256]{1,0:T(8,128)}, u32[]{:S(2)}, u32[]{:S(2)}) collective-permute-start(f32[1024,256]{1,0:T(8,128)} %get-tuple-element.210.down0), channel_id=1, source_target_pairs={{0,8},{8,0},{1,9},{9,1},{2,10},{10,2},{3,11},{11,3},{4,12},{12,4},... | collective-permute-start | bytes 3145736 | tf_op jit(solution)/shard_map/ppermute | solution.py:399
  531.9 17.6 %collective-permute-start.26 = (f32[64,1024]{1,0:T(8,128)}, f32[64,1024]{1,0:T(8,128)}, u32[]{:S(2)}, u32[]{:S(2)}) collective-permute-start(f32[64,1024]{1,0:T(8,128)} %get-tuple-element.179), channel_id=1, source_target_pairs={{0,4},{1,5},{2,6},{3,7},{4,0},{5,1},{6,2},{7,3},{8,12},{9,13},{10,... | collective-permute-start | bytes 786440 | tf_op jit(solution)/shard_map/ppermute | solution.py:347
  540.4 30.8 %collective-permute-start.27 = (f32[64,1024]{1,0:T(8,128)}, f32[64,1024]{1,0:T(8,128)}, u32[]{:S(2)}, u32[]{:S(2)}) collective-permute-start(f32[64,1024]{1,0:T(8,128)} %get-tuple-element.180), channel_id=1, source_target_pairs={{0,2},{1,3},{2,0},{3,1},{4,6},{5,7},{6,4},{7,5},{8,10},{9,11},{10,... | collective-permute-start | bytes 786440 | tf_op jit(solution)/shard_map/ppermute | solution.py:347
  541.7 30.9 %collective-permute-start.28 = (f32[64,1536]{1,0:T(8,128)}, f32[64,1536]{1,0:T(8,128)S(1)}, u32[]{:S(2)}, u32[]{:S(2)}) collective-permute-start(f32[64,1536]{1,0:T(8,128)} %get-tuple-element.181), channel_id=1, source_target_pairs={{0,4},{1,5},{2,6},{3,7},{4,0},{5,1},{6,2},{7,3},{8,12},{9,13},{10,... | collective-permute-start | bytes 1179656 | tf_op jit(solution)/shard_map/ppermute | solution.py:347
  547.5 25.8 %collective-permute-start.29 = (f32[64,1536]{1,0:T(8,128)}, f32[64,1536]{1,0:T(8,128)S(1)}, u32[]{:S(2)}, u32[]{:S(2)}) collective-permute-start(f32[64,1536]{1,0:T(8,128)} %get-tuple-element.182), channel_id=1, source_target_pairs={{0,2},{1,3},{2,0},{3,1},{4,6},{5,7},{6,4},{7,5},{8,10},{9,11},{10,... | collective-permute-start | bytes 1179656 | tf_op jit(solution)/shard_map/ppermute | solution.py:347
  548.5 25.7 %collective-permute-start.24 = (f32[2,64,1536]{2,1,0:T(8,128)}, f32[2,64,1536]{2,1,0:T(8,128)S(1)}, u32[]{:S(2)}, u32[]{:S(2)}) collective-permute-start(f32[2,64,1536]{2,1,0:T(8,128)} %get-tuple-element.177), channel_id=1, source_target_pairs={{0,2},{1,3},{2,0},{3,1},{4,6},{5,7},{6,4},{7,5},{8,10},{9,11},{10,... | collective-permute-start | bytes 2359304 | tf_op jit(solution)/shard_map/ppermute | solution.py:347
  549.5 24.7 %collective-permute-start.25 = (f32[2,64,1536]{2,1,0:T(8,128)}, f32[2,64,1536]{2,1,0:T(8,128)S(1)}, u32[]{:S(2)}, u32[]{:S(2)}) collective-permute-start(f32[2,64,1536]{2,1,0:T(8,128)} %get-tuple-element.178), channel_id=1, source_target_pairs={{0,4},{1,5},{2,6},{3,7},{4,0},{5,1},{6,2},{7,3},{8,12},{9,13},{10,... | collective-permute-start | bytes 2359304 | tf_op jit(solution)/shard_map/ppermute | solution.py:347
  550.7 22.5 %copy-start.32 = (f32[6,1024]{1,0:T(8,128)S(1)}, f32[6,1024]{1,0:T(8,128)}, u32[]{:S(2)}) copy-start(f32[6,1024]{1,0:T(8,128)} %slice.112) | copy-start | bytes 73732
  571.1 46.6 %collective-permute-start.42 = (f32[128,2048]{1,0:T(8,128)}, f32[128,2048]{1,0:T(8,128)}, u32[]{:S(2)}, u32[]{:S(2)}) collective-permute-start(f32[128,2048]{1,0:T(8,128)} %get-tuple-element.209.up1), channel_id=1, source_target_pairs={{0,8},{8,0},{1,9},{9,1},{2,10},{10,2},{3,11},{11,3},{4,12},{12,4},... | collective-permute-start | bytes 3145736 | tf_op jit(solution)/shard_map/ppermute | solution.py:399
  572.6 46.8 %collective-permute-start.43 = (f32[1024,256]{1,0:T(8,128)}, f32[1024,256]{1,0:T(8,128)}, u32[]{:S(2)}, u32[]{:S(2)}) collective-permute-start(f32[1024,256]{1,0:T(8,128)} %get-tuple-element.212.down1), channel_id=1, source_target_pairs={{0,8},{8,0},{1,9},{9,1},{2,10},{10,2},{3,11},{11,3},{4,12},{12,4},... | collective-permute-start | bytes 3145736 | tf_op jit(solution)/shard_map/ppermute | solution.py:399
  581.8 9.1 %collective-permute-start.34 = (f32[64,1536]{1,0:T(8,128)}, f32[64,1536]{1,0:T(8,128)S(1)}, u32[]{:S(2)}, u32[]{:S(2)}) collective-permute-start(f32[64,1536]{1,0:T(8,128)} %get-tuple-element.194), channel_id=1, source_target_pairs={{0,4},{1,5},{2,6},{3,7},{4,0},{5,1},{6,2},{7,3},{8,12},{9,13},{10,... | collective-permute-start | bytes 1179656 | tf_op jit(solution)/shard_map/ppermute | solution.py:347
  582.5 8.5 %collective-permute-start.35 = (f32[64,1536]{1,0:T(8,128)}, f32[64,1536]{1,0:T(8,128)S(1)}, u32[]{:S(2)}, u32[]{:S(2)}) collective-permute-start(f32[64,1536]{1,0:T(8,128)} %get-tuple-element.195), channel_id=1, source_target_pairs={{0,2},{1,3},{2,0},{3,1},{4,6},{5,7},{6,4},{7,5},{8,10},{9,11},{10,... | collective-permute-start | bytes 1179656 | tf_op jit(solution)/shard_map/ppermute | solution.py:347
  583.4 14.5 %copy-start.28 = (f32[64,1024]{1,0:T(8,128)S(1)}, f32[64,1024]{1,0:T(8,128)}, u32[]{:S(2)}) copy-start(f32[64,1024]{1,0:T(8,128)} %get-tuple-element.190.refs_0_) | copy-start | bytes 786436
  583.4 1.4 collective-permute-start.36
  597.0 4.5 collective-permute-start.39
  597.9 42.5 %collective-permute-start.30 = (f32[64,1024]{1,0:T(8,128)S(1)}, f32[64,1024]{1,0:T(8,128)}, u32[]{:S(2)}, u32[]{:S(2)}) collective-permute-start(f32[64,1024]{1,0:T(8,128)S(1)} %copy-done.28), channel_id=1, source_target_pairs={{0,8},{8,0},{1,9},{9,1},{2,10},{10,2},{3,11},{11,3},{4,12},{12,4},... | collective-permute-start | bytes 786440 | tf_op jit(solution)/shard_map/ppermute | solution.py:399
  605.7 6.6 collective-permute-start.40
  616.3 22.9 %collective-permute-start.41 = (f32[64,128]{1,0:T(8,128)}, f32[64,128]{1,0:T(8,128)}, u32[]{:S(2)}, u32[]{:S(2)}) collective-permute-start(f32[64,128]{1,0:T(8,128)} %moves.19), channel_id=1, source_target_pairs={{0,8},{8,0},{1,9},{9,1},{2,10},{10,2},{3,11},{11,3},{4,12},{12,4},... | collective-permute-start | bytes 98312 | tf_op jit(solution)/shard_map/ppermute | solution.py:399
  635.5 9.2 %collective-permute-start.31 = (f32[64,1024]{1,0:T(8,128)S(1)}, f32[64,1024]{1,0:T(8,128)S(1)}, u32[]{:S(2)}, u32[]{:S(2)}) collective-permute-start(f32[64,1024]{1,0:T(8,128)S(1)} %copy-done.29), channel_id=1, source_target_pairs={{0,8},{8,0},{1,9},{9,1},{2,10},{10,2},{3,11},{11,3},{4,12},{12,4},... | collective-permute-start | bytes 786440 | tf_op jit(solution)/shard_map/ppermute | solution.py:399
  637.1 16.0 %collective-permute-start.32 = (f32[64,1536]{1,0:T(8,128)S(1)}, f32[64,1536]{1,0:T(8,128)S(1)}, u32[]{:S(2)}, u32[]{:S(2)}) collective-permute-start(f32[64,1536]{1,0:T(8,128)S(1)} %copy-done.17), channel_id=1, source_target_pairs={{0,8},{8,0},{1,9},{9,1},{2,10},{10,2},{3,11},{11,3},{4,12},{12,4},... | collective-permute-start | bytes 1179656 | tf_op jit(solution)/shard_map/ppermute | solution.py:399
  637.5 24.0 %collective-permute-start.33 = (f32[64,1536]{1,0:T(8,128)S(1)}, f32[64,1536]{1,0:T(8,128)S(1)}, u32[]{:S(2)}, u32[]{:S(2)}) collective-permute-start(f32[64,1536]{1,0:T(8,128)S(1)} %copy-done.18), channel_id=1, source_target_pairs={{0,8},{8,0},{1,9},{9,1},{2,10},{10,2},{3,11},{11,3},{4,12},{12,4},... | collective-permute-start | bytes 1179656 | tf_op jit(solution)/shard_map/ppermute | solution.py:399
  639.1 27.9 %collective-permute-start.37 = (f32[64,1536]{1,0:T(8,128)S(1)}, f32[64,1536]{1,0:T(8,128)S(1)}, u32[]{:S(2)}, u32[]{:S(2)}) collective-permute-start(f32[64,1536]{1,0:T(8,128)S(1)} %copy-done.19), channel_id=1, source_target_pairs={{0,8},{8,0},{1,9},{9,1},{2,10},{10,2},{3,11},{11,3},{4,12},{12,4},... | collective-permute-start | bytes 1179656 | tf_op jit(solution)/shard_map/ppermute | solution.py:399
  640.3 30.9 %collective-permute-start.38 = (f32[64,1536]{1,0:T(8,128)S(1)}, f32[64,1536]{1,0:T(8,128)S(1)}, u32[]{:S(2)}, u32[]{:S(2)}) collective-permute-start(f32[64,1536]{1,0:T(8,128)S(1)} %copy-done.20), channel_id=1, source_target_pairs={{0,8},{8,0},{1,9},{9,1},{2,10},{10,2},{3,11},{11,3},{4,12},{12,4},... | collective-permute-start | bytes 1179656 | tf_op jit(solution)/shard_map/ppermute | solution.py:399
  644.7 22.3 %copy-start.30 = (f32[64,1024]{1,0:T(8,128)}, f32[64,1024]{1,0:T(8,128)S(1)}, u32[]{:S(2)}) copy-start(f32[64,1024]{1,0:T(8,128)S(1)} %collective-permute-done.31.refs_3_) | copy-start | bytes 786436
  653.1 18.1 %copy-start.21 = (f32[64,1536]{1,0:T(8,128)}, f32[64,1536]{1,0:T(8,128)S(1)}, u32[]{:S(2)}) copy-start(f32[64,1536]{1,0:T(8,128)S(1)} %collective-permute-done.32.refs_5_) | copy-start | bytes 1179652
  (40 other events, 199.2 us)
Sparse Core Ops, SparseCore 0:
  11.6 53.4 all-gather.6
  67.5 50.6 all-gather.8
  120.7 50.5 all-gather.10
